TPU v7x, 8 devices: a whole 2x2x1 slice. The times are simulated.
8 devices in a mesh: batch: 1 (over z), cols: 2 (over y), rows: 4 (over x, core).
Axes of the slice: x: 2, y: 2, z: 1, core: 2. Of those that a mesh axis runs over, the one named last changes fastest.
Arguments:
- frames: bfloat16 [4, 2, 64, 16, 384], P(None, 'batch', 'rows', 'cols')
- w_x: bfloat16 [3, 3, 384, 1536], replicated
- w_h: bfloat16 [3, 3, 384, 1536], replicated
- gate_bias: float32 [1536], replicated
- h_init: bfloat16 [2, 64, 16, 384], P('batch', 'rows', 'cols')
- c_init: float32 [2, 64, 16, 384], P('batch', 'rows', 'cols')
Outputs:
- output 1: bfloat16 [4, 2, 64, 16, 384], P(None, 'batch', 'rows', 'cols')
- output 2: float32 [2, 64, 16, 384], P('batch', 'rows', 'cols')
All inputs are finite; a program needn't handle non-finite values.
Results may differ from a plain program's by a relative error of at most 0.001.
Values are sent between devices in bfloat16 or wider.
A program may use at most 1 GiB of HBM per device.

v0:
```python
import jax
import jax.numpy as jnp
from jax import lax
from jax.sharding import PartitionSpec as P, NamedSharding


def edge_swap(tile_arr, halo_width, split_dim, axis_label, axis_count):
    length = tile_arr.shape[split_dim]
    low_edge = lax.slice_in_dim(tile_arr, 0, halo_width, axis=split_dim)
    high_edge = lax.slice_in_dim(tile_arr, length - halo_width, length, axis=split_dim)
    down_pairs = [(source, source + 1) for source in range(axis_count - 1)]
    up_pairs = [(source + 1, source) for source in range(axis_count - 1)]
    from_prev = lax.ppermute(high_edge, axis_label, down_pairs)
    from_next = lax.ppermute(low_edge, axis_label, up_pairs)
    return jnp.concatenate([from_prev, tile_arr, from_next], axis=split_dim)


def with_halo(tile_arr, halo_width, row_dim, row_count, col_count):
    row_ext = edge_swap(tile_arr, halo_width, row_dim, "rows", row_count)
    return edge_swap(row_ext, halo_width, row_dim + 1, "cols", col_count)


def conv_taps(padded, weights, out_rows, out_cols):
    tap_list = [padded[:, row_off:row_off + out_rows, col_off:col_off + out_cols, :] for row_off in range(3) for col_off in range(3)]
    patches = jnp.concatenate(tap_list, axis=-1)
    flat_patches = patches.reshape(-1, patches.shape[-1])
    flat_weights = weights.reshape(-1, weights.shape[-1])
    product = jnp.dot(flat_patches, flat_weights, preferred_element_type=jnp.float32)
    return product.reshape(padded.shape[0], out_rows, out_cols, -1)


def lstm_cell(gate_sum, cell_prev):
    hidden_width = cell_prev.shape[-1]
    in_gate = jax.nn.sigmoid(gate_sum[..., :hidden_width])
    forget_gate = jax.nn.sigmoid(gate_sum[..., hidden_width:2 * hidden_width])
    out_gate = jax.nn.sigmoid(gate_sum[..., 2 * hidden_width:3 * hidden_width])
    cand_gate = jnp.tanh(gate_sum[..., 3 * hidden_width:])
    cell_next = forget_gate * cell_prev + in_gate * cand_gate
    hidden_next = (out_gate * jnp.tanh(cell_next)).astype(jnp.bfloat16)
    return hidden_next, cell_next


def solution(mesh):
    row_count = mesh.shape["rows"]
    col_count = mesh.shape["cols"]
    frame_spec = P(None, "batch", "rows", "cols", None)
    state_spec = P("batch", "rows", "cols", None)

    def local_run(frames, w_x, w_h, gate_bias, h_init, c_init):
        tile_rows = h_init.shape[1]
        tile_cols = h_init.shape[2]
        frames_ext = with_halo(frames, 1, 2, row_count, col_count)

        def step_fn(state_pair, frame_ext):
            hidden, cell_state = state_pair
            hidden_ext = with_halo(hidden, 1, 1, row_count, col_count)
            gate_sum = conv_taps(frame_ext, w_x, tile_rows, tile_cols) + conv_taps(hidden_ext, w_h, tile_rows, tile_cols) + gate_bias
            hidden_next, cell_next = lstm_cell(gate_sum, cell_state)
            return (hidden_next, cell_next), hidden_next

        final_pair, all_hidden = lax.scan(step_fn, (h_init, c_init), frames_ext)
        return all_hidden, final_pair[1]

    return jax.shard_map(local_run, mesh=mesh, in_specs=(frame_spec, P(), P(), P(), state_spec, state_spec), out_specs=(frame_spec, state_spec), check_vma=False)
```

profile of v0, /device:TPU:0, one launch (start us, length us, event | category | flops | bytes accessed | tf_op | source)
XLA Modules:
  0.0 146.9 jit_solution(17291731042309302567)
XLA Ops:
  1.5 2.8 %collective-permute-start.4 = (bf16[4,2,1,8,384]{4,3,2,1,0:T(8,128)(2,1)S(1)}, bf16[4,2,1,8,384]{4,3,2,1,0:T(8,128)(2,1)S(1)}, u32[]{:S(2)}, u32[]{:S(2)}) collective-permute-start(bf16[4,2,1,8,384]{4,3,2,1,0:T(8,128)(2,1)S(1)} %get-tuple-element.73), channel_id=1, source_target_pairs={{0,1},{1,2},{2,3},{4,5},{5,6},{6,7}} | collective-permute-start | bytes 147464 | tf_op jit(solution)/shard_map/ppermute | solution.py:13
  5.8 3.7 %collective-permute-done.5 = bf16[4,2,1,8,384]{4,3,2,1,0:T(8,128)(2,1)S(1)} collective-permute-done((bf16[4,2,1,8,384]{4,3,2,1,0:T(8,128)(2,1)S(1)}, bf16[4,2,1,8,384]{4,3,2,1,0:T(8,128)(2,1)S(1)}, u32[]{:S(2)}, u32[]{:S(2)}) %collective-permute-start.5) | collective-permute-done | bytes 49184 | tf_op jit(solution)/shard_map/ppermute | solution.py:14
  9.9 3.6 %collective-permute-start.6 = (bf16[4,2,18,1,384]{4,3,2,1,0:T(2,128)(2,1)S(1)}, bf16[4,2,18,1,384]{4,3,2,1,0:T(2,128)(2,1)S(1)}, u32[]{:S(2)}, u32[]{:S(2)}) collective-permute-start(bf16[4,2,18,1,384]{4,3,2,1,0:T(2,128)(2,1)S(1)} %get-tuple-element.70), channel_id=1, source_target_pairs={{0,4},{1,5},{2,6},{3,7}} | collective-permute-start | bytes 331784 | tf_op jit(solution)/shard_map/ppermute | solution.py:13
  14.8 2.6 %collective-permute-done.6 = bf16[4,2,18,1,384]{4,3,2,1,0:T(2,128)(2,1)S(1)} collective-permute-done((bf16[4,2,18,1,384]{4,3,2,1,0:T(2,128)(2,1)S(1)}, bf16[4,2,18,1,384]{4,3,2,1,0:T(2,128)(2,1)S(1)}, u32[]{:S(2)}, u32[]{:S(2)}) %collective-permute-start.6) | collective-permute-done | bytes 110624 | tf_op jit(solution)/shard_map/ppermute | solution.py:13
  17.4 4.7 %collective-permute-done.7 = bf16[4,2,18,1,384]{4,3,2,1,0:T(2,128)(2,1)} collective-permute-done((bf16[4,2,18,1,384]{4,3,2,1,0:T(2,128)(2,1)S(1)}, bf16[4,2,18,1,384]{4,3,2,1,0:T(2,128)(2,1)}, u32[]{:S(2)}, u32[]{:S(2)}) %collective-permute-start.7) | collective-permute-done | bytes 110624 | tf_op jit(solution)/shard_map/ppermute | solution.py:14
  22.1 2.1 %pad_maximum_fusion.4 = bf16[4,2,18,10,384]{4,3,2,1,0:T(8,128)(2,1)S(1)} fusion(bf16[4,2,18,1,384]{4,3,2,1,0:T(2,128)(2,1)} %collective-permute-done.7, bf16[4,2,18,8,384]{4,3,2,1,0:T(8,128)(2,1)S(1)} %constant_dynamic-update-slice_fusion.4, bf16[4,2,18,1,384]{4,3,2,1,0:T(2,128)(2,1)S(1)} %collective-permute-done.6), kind=kLoop, calls=%fused_computation.59 | loop fusion | flops 3317760 | bytes 2211840 | tf_op jit(solution)/shard_map/concatenate | solution.py:15
  24.3 121.8 %while.14 = (s32[]{:T(128)}, bf16[2,16,8,384]{3,2,1,0:T(8,128)(2,1)S(1)}, f32[2,16,8,384]{3,2,1,0:T(8,128)S(1)}, bf16[4,2,16,8,384]{4,3,2,1,0:T(8,128)(2,1)}, bf...) while((s32[]{:T(128)}, ...), condition=%wide.region_1.2_spmd, body=%wide.region_0.1_spmd.sunk | while | flops 5441126400 | bytes 47570216 | solution.py:61
  24.3 3.3 %collective-permute-start = (bf16[2,1,8,384]{3,2,1,0:T(8,128)(2,1)S(1)}, bf16[2,1,8,384]{3,2,1,0:T(8,128)(2,1)S(1)}, u32[]{:S(2)}, u32[]{:S(2)}) collective-permute-start(bf16[2,1,8,384]{3,2,1,0:T(8,128)(2,1)S(1)} %get-tuple-element.130), channel_id=1, source_target_pairs={{0,1},{1,2},{2,3},{4,5},{5,6},{6,7}} | collective-permute-start | bytes 36872 | tf_op jit(solution)/shard_map/while/body/eval_jaxpr/ppermute | solution.py:13
  27.6 1.3 collective-permute-start.1
  30.8 1.6 %collective-permute-start.2 = (bf16[2,18,1,384]{3,2,1,0:T(2,128)(2,1)S(1)}, bf16[2,18,1,384]{3,2,1,0:T(2,128)(2,1)S(1)}, u32[]{:S(2)}, u32[]{:S(2)}) collective-permute-start(bf16[2,18,1,384]{3,2,1,0:T(2,128)(2,1)S(1)} %get-tuple-element.132), channel_id=1, source_target_pairs={{0,4},{1,5},{2,6},{3,7}} | collective-permute-start | bytes 82952 | tf_op jit(solution)/shard_map/while/body/eval_jaxpr/ppermute | solution.py:13
  32.5 8.3 %fusion.58 = f32[2,16,8,1536]{3,2,1,0:T(8,128)} fusion(bf16[2,16,8,3456]{3,2,1,0:T(8,128)(2,1)S(1)} %slice_dynamic-update-slice_fusion.26, bf16[3456,1536,1,1]{1,0,3,2:T(8,128)(2,1)} %bitcast.34), kind=kOutput, calls=%fused_computation.67.clone.1 | convolution fusion | flops 2717908992 | bytes 13959168 | tf_op jit(solution)/shard_map/while/body/eval_jaxpr/dot_general | solution.py:28
  42.2 4.6 %collective-permute-done.3 = bf16[2,18,1,384]{3,2,1,0:T(2,128)(2,1)S(1)} collective-permute-done((bf16[2,18,1,384]{3,2,1,0:T(2,128)(2,1)S(1)}, bf16[2,18,1,384]{3,2,1,0:T(2,128)(2,1)S(1)}, u32[]{:S(2)}, u32[]{:S(2)}) %collective-permute-start.3) | collective-permute-done | bytes 27680 | tf_op jit(solution)/shard_map/while/body/eval_jaxpr/ppermute | solution.py:14
  47.5 5.8 %fusion.69 = f32[2,16,8,1536]{3,2,1,0:T(8,128)S(1)} fusion(f32[2,16,8,1536]{3,2,1,0:T(8,128)S(1)} %copy-done.5, bf16[2,16,8,3456]{3,2,1,0:T(8,128)(2,1)S(1)} %fusion.68, bf16[3456,1536,1,1]{1,0,3,2:T(8,128)(2,1)} %bitcast.35, f32[1536]{0:T(1024)S(1)} %get-tuple-element.162), kind=kOutput, calls=%fused_computation.1.clone.1 | convolution fusion | flops 2718695424 | bytes 15538176 | tf_op jit(solution)/shard_map/while/body/eval_jaxpr/dot_general | solution.py:28
  54.5 2.8 %collective-permute-start = (bf16[2,1,8,384]{3,2,1,0:T(8,128)(2,1)S(1)}, bf16[2,1,8,384]{3,2,1,0:T(8,128)(2,1)S(1)}, u32[]{:S(2)}, u32[]{:S(2)}) collective-permute-start(bf16[2,1,8,384]{3,2,1,0:T(8,128)(2,1)S(1)} %get-tuple-element.130), channel_id=1, source_target_pairs={{0,1},{1,2},{2,3},{4,5},{5,6},{6,7}} | collective-permute-start | bytes 36872 | tf_op jit(solution)/shard_map/while/body/eval_jaxpr/ppermute | solution.py:13
  57.3 1.3 collective-permute-start.1
  59.3 1.9 %collective-permute-done.1 = bf16[2,1,8,384]{3,2,1,0:T(8,128)(2,1)S(1)} collective-permute-done((bf16[2,1,8,384]{3,2,1,0:T(8,128)(2,1)S(1)}, bf16[2,1,8,384]{3,2,1,0:T(8,128)(2,1)S(1)}, u32[]{:S(2)}, u32[]{:S(2)}) %collective-permute-start.1) | collective-permute-done | bytes 12320 | tf_op jit(solution)/shard_map/while/body/eval_jaxpr/ppermute | solution.py:14
  61.3 1.6 %collective-permute-start.2 = (bf16[2,18,1,384]{3,2,1,0:T(2,128)(2,1)S(1)}, bf16[2,18,1,384]{3,2,1,0:T(2,128)(2,1)S(1)}, u32[]{:S(2)}, u32[]{:S(2)}) collective-permute-start(bf16[2,18,1,384]{3,2,1,0:T(2,128)(2,1)S(1)} %get-tuple-element.132), channel_id=1, source_target_pairs={{0,4},{1,5},{2,6},{3,7}} | collective-permute-start | bytes 82952 | tf_op jit(solution)/shard_map/while/body/eval_jaxpr/ppermute | solution.py:13
  62.9 8.3 %fusion.58 = f32[2,16,8,1536]{3,2,1,0:T(8,128)} fusion(bf16[2,16,8,3456]{3,2,1,0:T(8,128)(2,1)S(1)} %slice_dynamic-update-slice_fusion.26, bf16[3456,1536,1,1]{1,0,3,2:T(8,128)(2,1)} %bitcast.34), kind=kOutput, calls=%fused_computation.67.clone.1 | convolution fusion | flops 2717908992 | bytes 13959168 | tf_op jit(solution)/shard_map/while/body/eval_jaxpr/dot_general | solution.py:28
  72.6 4.6 %collective-permute-done.3 = bf16[2,18,1,384]{3,2,1,0:T(2,128)(2,1)S(1)} collective-permute-done((bf16[2,18,1,384]{3,2,1,0:T(2,128)(2,1)S(1)}, bf16[2,18,1,384]{3,2,1,0:T(2,128)(2,1)S(1)}, u32[]{:S(2)}, u32[]{:S(2)}) %collective-permute-start.3) | collective-permute-done | bytes 27680 | tf_op jit(solution)/shard_map/while/body/eval_jaxpr/ppermute | solution.py:14
  78.0 5.8 %fusion.69 = f32[2,16,8,1536]{3,2,1,0:T(8,128)S(1)} fusion(f32[2,16,8,1536]{3,2,1,0:T(8,128)S(1)} %copy-done.5, bf16[2,16,8,3456]{3,2,1,0:T(8,128)(2,1)S(1)} %fusion.68, bf16[3456,1536,1,1]{1,0,3,2:T(8,128)(2,1)} %bitcast.35, f32[1536]{0:T(1024)S(1)} %get-tuple-element.162), kind=kOutput, calls=%fused_computation.1.clone.1 | convolution fusion | flops 2718695424 | bytes 15538176 | tf_op jit(solution)/shard_map/while/body/eval_jaxpr/dot_general | solution.py:28
  84.9 2.9 %collective-permute-start = (bf16[2,1,8,384]{3,2,1,0:T(8,128)(2,1)S(1)}, bf16[2,1,8,384]{3,2,1,0:T(8,128)(2,1)S(1)}, u32[]{:S(2)}, u32[]{:S(2)}) collective-permute-start(bf16[2,1,8,384]{3,2,1,0:T(8,128)(2,1)S(1)} %get-tuple-element.130), channel_id=1, source_target_pairs={{0,1},{1,2},{2,3},{4,5},{5,6},{6,7}} | collective-permute-start | bytes 36872 | tf_op jit(solution)/shard_map/while/body/eval_jaxpr/ppermute | solution.py:13
  89.8 2.0 %collective-permute-done.1 = bf16[2,1,8,384]{3,2,1,0:T(8,128)(2,1)S(1)} collective-permute-done((bf16[2,1,8,384]{3,2,1,0:T(8,128)(2,1)S(1)}, bf16[2,1,8,384]{3,2,1,0:T(8,128)(2,1)S(1)}, u32[]{:S(2)}, u32[]{:S(2)}) %collective-permute-start.1) | collective-permute-done | bytes 12320 | tf_op jit(solution)/shard_map/while/body/eval_jaxpr/ppermute | solution.py:14
  91.9 1.6 %collective-permute-start.2 = (bf16[2,18,1,384]{3,2,1,0:T(2,128)(2,1)S(1)}, bf16[2,18,1,384]{3,2,1,0:T(2,128)(2,1)S(1)}, u32[]{:S(2)}, u32[]{:S(2)}) collective-permute-start(bf16[2,18,1,384]{3,2,1,0:T(2,128)(2,1)S(1)} %get-tuple-element.132), channel_id=1, source_target_pairs={{0,4},{1,5},{2,6},{3,7}} | collective-permute-start | bytes 82952 | tf_op jit(solution)/shard_map/while/body/eval_jaxpr/ppermute | solution.py:13
  93.5 8.3 %fusion.58 = f32[2,16,8,1536]{3,2,1,0:T(8,128)} fusion(bf16[2,16,8,3456]{3,2,1,0:T(8,128)(2,1)S(1)} %slice_dynamic-update-slice_fusion.26, bf16[3456,1536,1,1]{1,0,3,2:T(8,128)(2,1)} %bitcast.34), kind=kOutput, calls=%fused_computation.67.clone.1 | convolution fusion | flops 2717908992 | bytes 13959168 | tf_op jit(solution)/shard_map/while/body/eval_jaxpr/dot_general | solution.py:28
  103.2 4.6 %collective-permute-done.3 = bf16[2,18,1,384]{3,2,1,0:T(2,128)(2,1)S(1)} collective-permute-done((bf16[2,18,1,384]{3,2,1,0:T(2,128)(2,1)S(1)}, bf16[2,18,1,384]{3,2,1,0:T(2,128)(2,1)S(1)}, u32[]{:S(2)}, u32[]{:S(2)}) %collective-permute-start.3) | collective-permute-done | bytes 27680 | tf_op jit(solution)/shard_map/while/body/eval_jaxpr/ppermute | solution.py:14
  108.6 5.8 %fusion.69 = f32[2,16,8,1536]{3,2,1,0:T(8,128)S(1)} fusion(f32[2,16,8,1536]{3,2,1,0:T(8,128)S(1)} %copy-done.5, bf16[2,16,8,3456]{3,2,1,0:T(8,128)(2,1)S(1)} %fusion.68, bf16[3456,1536,1,1]{1,0,3,2:T(8,128)(2,1)} %bitcast.35, f32[1536]{0:T(1024)S(1)} %get-tuple-element.162), kind=kOutput, calls=%fused_computation.1.clone.1 | convolution fusion | flops 2718695424 | bytes 15538176 | tf_op jit(solution)/shard_map/while/body/eval_jaxpr/dot_general | solution.py:28
  115.5 2.9 %collective-permute-start = (bf16[2,1,8,384]{3,2,1,0:T(8,128)(2,1)S(1)}, bf16[2,1,8,384]{3,2,1,0:T(8,128)(2,1)S(1)}, u32[]{:S(2)}, u32[]{:S(2)}) collective-permute-start(bf16[2,1,8,384]{3,2,1,0:T(8,128)(2,1)S(1)} %get-tuple-element.130), channel_id=1, source_target_pairs={{0,1},{1,2},{2,3},{4,5},{5,6},{6,7}} | collective-permute-start | bytes 36872 | tf_op jit(solution)/shard_map/while/body/eval_jaxpr/ppermute | solution.py:13
  120.4 2.0 %collective-permute-done.1 = bf16[2,1,8,384]{3,2,1,0:T(8,128)(2,1)S(1)} collective-permute-done((bf16[2,1,8,384]{3,2,1,0:T(8,128)(2,1)S(1)}, bf16[2,1,8,384]{3,2,1,0:T(8,128)(2,1)S(1)}, u32[]{:S(2)}, u32[]{:S(2)}) %collective-permute-start.1) | collective-permute-done | bytes 12320 | tf_op jit(solution)/shard_map/while/body/eval_jaxpr/ppermute | solution.py:14
  122.6 1.6 %collective-permute-start.2 = (bf16[2,18,1,384]{3,2,1,0:T(2,128)(2,1)S(1)}, bf16[2,18,1,384]{3,2,1,0:T(2,128)(2,1)S(1)}, u32[]{:S(2)}, u32[]{:S(2)}) collective-permute-start(bf16[2,18,1,384]{3,2,1,0:T(2,128)(2,1)S(1)} %get-tuple-element.132), channel_id=1, source_target_pairs={{0,4},{1,5},{2,6},{3,7}} | collective-permute-start | bytes 82952 | tf_op jit(solution)/shard_map/while/body/eval_jaxpr/ppermute | solution.py:13
  124.1 8.3 %fusion.58 = f32[2,16,8,1536]{3,2,1,0:T(8,128)} fusion(bf16[2,16,8,3456]{3,2,1,0:T(8,128)(2,1)S(1)} %slice_dynamic-update-slice_fusion.26, bf16[3456,1536,1,1]{1,0,3,2:T(8,128)(2,1)} %bitcast.34), kind=kOutput, calls=%fused_computation.67.clone.1 | convolution fusion | flops 2717908992 | bytes 13959168 | tf_op jit(solution)/shard_map/while/body/eval_jaxpr/dot_general | solution.py:28
  133.9 4.6 %collective-permute-done.3 = bf16[2,18,1,384]{3,2,1,0:T(2,128)(2,1)S(1)} collective-permute-done((bf16[2,18,1,384]{3,2,1,0:T(2,128)(2,1)S(1)}, bf16[2,18,1,384]{3,2,1,0:T(2,128)(2,1)S(1)}, u32[]{:S(2)}, u32[]{:S(2)}) %collective-permute-start.3) | collective-permute-done | bytes 27680 | tf_op jit(solution)/shard_map/while/body/eval_jaxpr/ppermute | solution.py:14
  139.2 5.8 %fusion.69 = f32[2,16,8,1536]{3,2,1,0:T(8,128)S(1)} fusion(f32[2,16,8,1536]{3,2,1,0:T(8,128)S(1)} %copy-done.5, bf16[2,16,8,3456]{3,2,1,0:T(8,128)(2,1)S(1)} %fusion.68, bf16[3456,1536,1,1]{1,0,3,2:T(8,128)(2,1)} %bitcast.35, f32[1536]{0:T(1024)S(1)} %get-tuple-element.162), kind=kOutput, calls=%fused_computation.1.clone.1 | convolution fusion | flops 2718695424 | bytes 15538176 | tf_op jit(solution)/shard_map/while/body/eval_jaxpr/dot_general | solution.py:28
  (142 shorter events, 24.4 us)
Async XLA Ops:
  0.6 5.0 %copy-start.3 = (bf16[4,2,16,8,384]{4,3,2,1,0:T(8,128)(2,1)S(1)}, bf16[4,2,16,8,384]{4,3,2,1,0:T(8,128)(2,1)}, u32[]{:S(2)}) copy-start(bf16[4,2,16,8,384]{4,3,2,1,0:T(8,128)(2,1)} %param.8) | copy-start | bytes 2359300
  1.5 4.1 %collective-permute-start.4 = (bf16[4,2,1,8,384]{4,3,2,1,0:T(8,128)(2,1)S(1)}, bf16[4,2,1,8,384]{4,3,2,1,0:T(8,128)(2,1)S(1)}, u32[]{:S(2)}, u32[]{:S(2)}) collective-permute-start(bf16[4,2,1,8,384]{4,3,2,1,0:T(8,128)(2,1)S(1)} %get-tuple-element.73), channel_id=1, source_target_pairs={{0,1},{1,2},{2,3},{4,5},{5,6},{6,7}} | collective-permute-start | bytes 147464 | tf_op jit(solution)/shard_map/ppermute | solution.py:13
  4.3 5.2 %collective-permute-start.5 = (bf16[4,2,1,8,384]{4,3,2,1,0:T(8,128)(2,1)S(1)}, bf16[4,2,1,8,384]{4,3,2,1,0:T(8,128)(2,1)S(1)}, u32[]{:S(2)}, u32[]{:S(2)}) collective-permute-start(bf16[4,2,1,8,384]{4,3,2,1,0:T(8,128)(2,1)S(1)} %get-tuple-element.72), channel_id=1, source_target_pairs={{1,0},{2,1},{3,2},{5,4},{6,5},{7,6}} | collective-permute-start | bytes 147464 | tf_op jit(solution)/shard_map/ppermute | solution.py:14
  9.9 14.4 %copy-start = (bf16[2,16,8,384]{3,2,1,0:T(8,128)(2,1)S(1)}, bf16[2,16,8,384]{3,2,1,0:T(8,128)(2,1)}, u32[]{:S(2)}) copy-start(bf16[2,16,8,384]{3,2,1,0:T(8,128)(2,1)} %param.12) | copy-start | bytes 589828
  9.9 14.4 %copy-start.2 = (f32[2,16,8,384]{3,2,1,0:T(8,128)S(1)}, f32[2,16,8,384]{3,2,1,0:T(8,128)}, u32[]{:S(2)}) copy-start(f32[2,16,8,384]{3,2,1,0:T(8,128)} %param.13) | copy-start | bytes 1179652
  9.9 14.4 %copy-start.4 = (f32[1536]{0:T(1024)S(1)}, f32[1536]{0:T(1024)}, u32[]{:S(2)}) copy-start(f32[1536]{0:T(1024)} %param.11) | copy-start | bytes 18436
  9.9 7.5 %collective-permute-start.6 = (bf16[4,2,18,1,384]{4,3,2,1,0:T(2,128)(2,1)S(1)}, bf16[4,2,18,1,384]{4,3,2,1,0:T(2,128)(2,1)S(1)}, u32[]{:S(2)}, u32[]{:S(2)}) collective-permute-start(bf16[4,2,18,1,384]{4,3,2,1,0:T(2,128)(2,1)S(1)} %get-tuple-element.70), channel_id=1, source_target_pairs={{0,4},{1,5},{2,6},{3,7}} | collective-permute-start | bytes 331784 | tf_op jit(solution)/shard_map/ppermute | solution.py:13
  13.5 8.7 %collective-permute-start.7 = (bf16[4,2,18,1,384]{4,3,2,1,0:T(2,128)(2,1)S(1)}, bf16[4,2,18,1,384]{4,3,2,1,0:T(2,128)(2,1)}, u32[]{:S(2)}, u32[]{:S(2)}) collective-permute-start(bf16[4,2,18,1,384]{4,3,2,1,0:T(2,128)(2,1)S(1)} %get-tuple-element.71), channel_id=1, source_target_pairs={{4,0},{5,1},{6,2},{7,3}} | collective-permute-start | bytes 331784 | tf_op jit(solution)/shard_map/ppermute | solution.py:14
  24.3 5.2 %collective-permute-start = (bf16[2,1,8,384]{3,2,1,0:T(8,128)(2,1)S(1)}, bf16[2,1,8,384]{3,2,1,0:T(8,128)(2,1)S(1)}, u32[]{:S(2)}, u32[]{:S(2)}) collective-permute-start(bf16[2,1,8,384]{3,2,1,0:T(8,128)(2,1)S(1)} %get-tuple-element.130), channel_id=1, source_target_pairs={{0,1},{1,2},{2,3},{4,5},{5,6},{6,7}} | collective-permute-start | bytes 36872 | tf_op jit(solution)/shard_map/while/body/eval_jaxpr/ppermute | solution.py:13
  27.6 3.2 %collective-permute-start.1 = (bf16[2,1,8,384]{3,2,1,0:T(8,128)(2,1)S(1)}, bf16[2,1,8,384]{3,2,1,0:T(8,128)(2,1)S(1)}, u32[]{:S(2)}, u32[]{:S(2)}) collective-permute-start(bf16[2,1,8,384]{3,2,1,0:T(8,128)(2,1)S(1)} %get-tuple-element.131), channel_id=1, source_target_pairs={{1,0},{2,1},{3,2},{5,4},{6,5},{7,6}} | collective-permute-start | bytes 36872 | tf_op jit(solution)/shard_map/while/body/eval_jaxpr/ppermute | solution.py:14
  30.8 11.2 %collective-permute-start.2 = (bf16[2,18,1,384]{3,2,1,0:T(2,128)(2,1)S(1)}, bf16[2,18,1,384]{3,2,1,0:T(2,128)(2,1)S(1)}, u32[]{:S(2)}, u32[]{:S(2)}) collective-permute-start(bf16[2,18,1,384]{3,2,1,0:T(2,128)(2,1)S(1)} %get-tuple-element.132), channel_id=1, source_target_pairs={{0,4},{1,5},{2,6},{3,7}} | collective-permute-start | bytes 82952 | tf_op jit(solution)/shard_map/while/body/eval_jaxpr/ppermute | solution.py:13
  40.7 6.0 %collective-permute-start.3 = (bf16[2,18,1,384]{3,2,1,0:T(2,128)(2,1)S(1)}, bf16[2,18,1,384]{3,2,1,0:T(2,128)(2,1)S(1)}, u32[]{:S(2)}, u32[]{:S(2)}) collective-permute-start(bf16[2,18,1,384]{3,2,1,0:T(2,128)(2,1)S(1)} %get-tuple-element.133), channel_id=1, source_target_pairs={{4,0},{5,1},{6,2},{7,3}} | collective-permute-start | bytes 82952 | tf_op jit(solution)/shard_map/while/body/eval_jaxpr/ppermute | solution.py:14
  42.1 5.4 %copy-start.5 = (f32[2,16,8,1536]{3,2,1,0:T(8,128)S(1)}, f32[2,16,8,1536]{3,2,1,0:T(8,128)}, u32[]{:S(2)}) copy-start(f32[2,16,8,1536]{3,2,1,0:T(8,128)} %fusion.58) | copy-start | bytes 4718596 | tf_op jit(solution)/shard_map/while
  54.5 4.8 %collective-permute-start = (bf16[2,1,8,384]{3,2,1,0:T(8,128)(2,1)S(1)}, bf16[2,1,8,384]{3,2,1,0:T(8,128)(2,1)S(1)}, u32[]{:S(2)}, u32[]{:S(2)}) collective-permute-start(bf16[2,1,8,384]{3,2,1,0:T(8,128)(2,1)S(1)} %get-tuple-element.130), channel_id=1, source_target_pairs={{0,1},{1,2},{2,3},{4,5},{5,6},{6,7}} | collective-permute-start | bytes 36872 | tf_op jit(solution)/shard_map/while/body/eval_jaxpr/ppermute | solution.py:13
  57.3 3.9 %collective-permute-start.1 = (bf16[2,1,8,384]{3,2,1,0:T(8,128)(2,1)S(1)}, bf16[2,1,8,384]{3,2,1,0:T(8,128)(2,1)S(1)}, u32[]{:S(2)}, u32[]{:S(2)}) collective-permute-start(bf16[2,1,8,384]{3,2,1,0:T(8,128)(2,1)S(1)} %get-tuple-element.131), channel_id=1, source_target_pairs={{1,0},{2,1},{3,2},{5,4},{6,5},{7,6}} | collective-permute-start | bytes 36872 | tf_op jit(solution)/shard_map/while/body/eval_jaxpr/ppermute | solution.py:14
  61.3 11.2 %collective-permute-start.2 = (bf16[2,18,1,384]{3,2,1,0:T(2,128)(2,1)S(1)}, bf16[2,18,1,384]{3,2,1,0:T(2,128)(2,1)S(1)}, u32[]{:S(2)}, u32[]{:S(2)}) collective-permute-start(bf16[2,18,1,384]{3,2,1,0:T(2,128)(2,1)S(1)} %get-tuple-element.132), channel_id=1, source_target_pairs={{0,4},{1,5},{2,6},{3,7}} | collective-permute-start | bytes 82952 | tf_op jit(solution)/shard_map/while/body/eval_jaxpr/ppermute | solution.py:13
  71.2 6.0 %collective-permute-start.3 = (bf16[2,18,1,384]{3,2,1,0:T(2,128)(2,1)S(1)}, bf16[2,18,1,384]{3,2,1,0:T(2,128)(2,1)S(1)}, u32[]{:S(2)}, u32[]{:S(2)}) collective-permute-start(bf16[2,18,1,384]{3,2,1,0:T(2,128)(2,1)S(1)} %get-tuple-element.133), channel_id=1, source_target_pairs={{4,0},{5,1},{6,2},{7,3}} | collective-permute-start | bytes 82952 | tf_op jit(solution)/shard_map/while/body/eval_jaxpr/ppermute | solution.py:14
  72.6 5.4 %copy-start.5 = (f32[2,16,8,1536]{3,2,1,0:T(8,128)S(1)}, f32[2,16,8,1536]{3,2,1,0:T(8,128)}, u32[]{:S(2)}) copy-start(f32[2,16,8,1536]{3,2,1,0:T(8,128)} %fusion.58) | copy-start | bytes 4718596 | tf_op jit(solution)/shard_map/while
  84.9 4.9 %collective-permute-start = (bf16[2,1,8,384]{3,2,1,0:T(8,128)(2,1)S(1)}, bf16[2,1,8,384]{3,2,1,0:T(8,128)(2,1)S(1)}, u32[]{:S(2)}, u32[]{:S(2)}) collective-permute-start(bf16[2,1,8,384]{3,2,1,0:T(8,128)(2,1)S(1)} %get-tuple-element.130), channel_id=1, source_target_pairs={{0,1},{1,2},{2,3},{4,5},{5,6},{6,7}} | collective-permute-start | bytes 36872 | tf_op jit(solution)/shard_map/while/body/eval_jaxpr/ppermute | solution.py:13
  87.8 4.0 %collective-permute-start.1 = (bf16[2,1,8,384]{3,2,1,0:T(8,128)(2,1)S(1)}, bf16[2,1,8,384]{3,2,1,0:T(8,128)(2,1)S(1)}, u32[]{:S(2)}, u32[]{:S(2)}) collective-permute-start(bf16[2,1,8,384]{3,2,1,0:T(8,128)(2,1)S(1)} %get-tuple-element.131), channel_id=1, source_target_pairs={{1,0},{2,1},{3,2},{5,4},{6,5},{7,6}} | collective-permute-start | bytes 36872 | tf_op jit(solution)/shard_map/while/body/eval_jaxpr/ppermute | solution.py:14
  91.9 11.2 %collective-permute-start.2 = (bf16[2,18,1,384]{3,2,1,0:T(2,128)(2,1)S(1)}, bf16[2,18,1,384]{3,2,1,0:T(2,128)(2,1)S(1)}, u32[]{:S(2)}, u32[]{:S(2)}) collective-permute-start(bf16[2,18,1,384]{3,2,1,0:T(2,128)(2,1)S(1)} %get-tuple-element.132), channel_id=1, source_target_pairs={{0,4},{1,5},{2,6},{3,7}} | collective-permute-start | bytes 82952 | tf_op jit(solution)/shard_map/while/body/eval_jaxpr/ppermute | solution.py:13
  101.8 6.0 %collective-permute-start.3 = (bf16[2,18,1,384]{3,2,1,0:T(2,128)(2,1)S(1)}, bf16[2,18,1,384]{3,2,1,0:T(2,128)(2,1)S(1)}, u32[]{:S(2)}, u32[]{:S(2)}) collective-permute-start(bf16[2,18,1,384]{3,2,1,0:T(2,128)(2,1)S(1)} %get-tuple-element.133), channel_id=1, source_target_pairs={{4,0},{5,1},{6,2},{7,3}} | collective-permute-start | bytes 82952 | tf_op jit(solution)/shard_map/while/body/eval_jaxpr/ppermute | solution.py:14
  103.2 5.4 %copy-start.5 = (f32[2,16,8,1536]{3,2,1,0:T(8,128)S(1)}, f32[2,16,8,1536]{3,2,1,0:T(8,128)}, u32[]{:S(2)}) copy-start(f32[2,16,8,1536]{3,2,1,0:T(8,128)} %fusion.58) | copy-start | bytes 4718596 | tf_op jit(solution)/shard_map/while
  115.5 4.9 %collective-permute-start = (bf16[2,1,8,384]{3,2,1,0:T(8,128)(2,1)S(1)}, bf16[2,1,8,384]{3,2,1,0:T(8,128)(2,1)S(1)}, u32[]{:S(2)}, u32[]{:S(2)}) collective-permute-start(bf16[2,1,8,384]{3,2,1,0:T(8,128)(2,1)S(1)} %get-tuple-element.130), channel_id=1, source_target_pairs={{0,1},{1,2},{2,3},{4,5},{5,6},{6,7}} | collective-permute-start | bytes 36872 | tf_op jit(solution)/shard_map/while/body/eval_jaxpr/ppermute | solution.py:13
  118.4 4.0 %collective-permute-start.1 = (bf16[2,1,8,384]{3,2,1,0:T(8,128)(2,1)S(1)}, bf16[2,1,8,384]{3,2,1,0:T(8,128)(2,1)S(1)}, u32[]{:S(2)}, u32[]{:S(2)}) collective-permute-start(bf16[2,1,8,384]{3,2,1,0:T(8,128)(2,1)S(1)} %get-tuple-element.131), channel_id=1, source_target_pairs={{1,0},{2,1},{3,2},{5,4},{6,5},{7,6}} | collective-permute-start | bytes 36872 | tf_op jit(solution)/shard_map/while/body/eval_jaxpr/ppermute | solution.py:14
  122.6 11.2 %collective-permute-start.2 = (bf16[2,18,1,384]{3,2,1,0:T(2,128)(2,1)S(1)}, bf16[2,18,1,384]{3,2,1,0:T(2,128)(2,1)S(1)}, u32[]{:S(2)}, u32[]{:S(2)}) collective-permute-start(bf16[2,18,1,384]{3,2,1,0:T(2,128)(2,1)S(1)} %get-tuple-element.132), channel_id=1, source_target_pairs={{0,4},{1,5},{2,6},{3,7}} | collective-permute-start | bytes 82952 | tf_op jit(solution)/shard_map/while/body/eval_jaxpr/ppermute | solution.py:13
  132.4 6.0 %collective-permute-start.3 = (bf16[2,18,1,384]{3,2,1,0:T(2,128)(2,1)S(1)}, bf16[2,18,1,384]{3,2,1,0:T(2,128)(2,1)S(1)}, u32[]{:S(2)}, u32[]{:S(2)}) collective-permute-start(bf16[2,18,1,384]{3,2,1,0:T(2,128)(2,1)S(1)} %get-tuple-element.133), channel_id=1, source_target_pairs={{4,0},{5,1},{6,2},{7,3}} | collective-permute-start | bytes 82952 | tf_op jit(solution)/shard_map/while/body/eval_jaxpr/ppermute | solution.py:14
  133.8 5.4 %copy-start.5 = (f32[2,16,8,1536]{3,2,1,0:T(8,128)S(1)}, f32[2,16,8,1536]{3,2,1,0:T(8,128)}, u32[]{:S(2)}) copy-start(f32[2,16,8,1536]{3,2,1,0:T(8,128)} %fusion.58) | copy-start | bytes 4718596 | tf_op jit(solution)/shard_map/while
  146.1 0.7 copy-start.1
where the time goes:
time: 148 us; the launch traced here: 147 us
  matrix products  56.3 us (38%)
  starting transfers between devices  37.5 us (25%)
  waiting for transfers between devices  36.5 us (25%)
  other arithmetic  9.83 us (7%)
  local copies, waits for them, and re-layouts  5.25 us (4%)
    dot_general x8, matrix products, conv_taps(): jnp.dot(flat_patches, flat_weights, preferred_element_type=jnp.float32)  56.3 us
    ppermute x10, waiting for transfers between devices, edge_swap(): from_next = lax.ppermute(low_edge, axis_label, up_pairs)  33.9 us
    ppermute x10, starting transfers between devices, edge_swap(): from_prev = lax.ppermute(high_edge, axis_label, down_pairs)  24.6 us
    ppermute x10, starting transfers between devices, edge_swap(): from_next = lax.ppermute(low_edge, axis_label, up_pairs)  12.9 us
    dynamic_update_slice x4, other arithmetic, local_run(): final_pair, all_hidden = lax.scan(step_fn, (h_init, c_init), frames_ext)  4.45 us
  transfers between devices with their start and end apart: 20, of which 11 were waited for; matrix products, arithmetic and copies ran while one was open for 25% of the time, Pallas kernels for 0%

commit v1 on v0

v1 whole, which is shorter than its diff:
```python
import functools

import jax
import jax.numpy as jnp
from jax import lax
from jax.experimental import pallas as pl
from jax.experimental.pallas import tpu as pltpu
from jax.sharding import PartitionSpec as P

MESH = pl.DeviceIdType.MESH
BF16 = jnp.bfloat16
F32 = jnp.float32

STEPS = 4
SEQS = 2
ROWS = 16
COLS = 8
CH = 384
LANES = 128
CHUNKS = CH // LANES
TAP_ROWS = 3 * CH
DEPTH = 3 * TAP_ROWS
GATES = 4 * CH
CELLS = ROWS * SEQS * COLS
PITCH = 16
GROUPS = (ROWS + 2) * SEQS
STAGE_ROWS = GROUPS * PITCH + 8


def sigmoid(value):
    return 0.5 * jnp.tanh(0.5 * value) + 0.5


def im2col(taps):
    return jnp.concatenate([taps[d * 16 : d * 16 + CELLS, :] for d in range(3)], axis=1)


def gate_columns(weights, block):
    return jnp.concatenate([weights[:, g * CH + block * LANES : g * CH + (block + 1) * LANES] for g in range(4)], axis=1)


def kernel(
    row_count,
    frames_hbm, wx_hbm, wh_hbm, bias_ref, h_hbm, c_hbm,
    out_hbm, c_out_hbm,
    wx, wh, frames, hidden, cell, xtaps, htaps, gate_x, stage,
    send_col, send_cor, recv_row, recv_col, recv_cor,
    in_sem, w_sem, out_sem, send_sem, recv_sem,
):
    row = lax.axis_index("rows")
    col = lax.axis_index("cols")
    other = 1 - col
    has_up = row > 0
    has_down = row < row_count - 1
    first_col = col == 0

    loads = []
    for t in range(STEPS):
        loads.append([pltpu.make_async_copy(frames_hbm.at[t, s], frames.at[t, :, s], in_sem.at[t, s]) for s in range(SEQS)])
    loads.append([pltpu.make_async_copy(h_hbm.at[s], hidden.at[0, :, s], in_sem.at[STEPS, s]) for s in range(SEQS)])
    loads.append([pltpu.make_async_copy(c_hbm.at[s], cell.at[:, s], in_sem.at[STEPS + 1, s]) for s in range(SEQS)])
    w_loads = [pltpu.make_async_copy(src, dst, w_sem.at[i]) for i, (src, dst) in enumerate(((wx_hbm, wx), (wh_hbm, wh)))]
    for group in (loads[0], loads[STEPS], loads[1], loads[2], loads[3]):
        for copy in group:
            copy.start()
    w_loads[0].start()
    for copy in loads[STEPS + 1]:
        copy.start()
    w_loads[1].start()

    recv_row[...] = jnp.zeros_like(recv_row)
    recv_cor[...] = jnp.zeros_like(recv_cor)

    barrier = pltpu.get_barrier_semaphore()

    def greet(r, c):
        pl.semaphore_signal(barrier, inc=1, device_id={"rows": r, "cols": c}, device_id_type=MESH)

    greet(row, other)

    @pl.when(has_up)
    def _():
        greet(row - 1, col)
        greet(row - 1, other)

    @pl.when(has_down)
    def _():
        greet(row + 1, col)
        greet(row + 1, other)

    inner = jnp.logical_and(has_up, has_down)

    @pl.when(inner)
    def _():
        pl.semaphore_wait(barrier, 5)

    @pl.when(jnp.logical_not(inner))
    def _():
        pl.semaphore_wait(barrier, 3)

    def tile_ref(field):
        return frames.at[field] if field < STEPS else hidden.at[field - STEPS]

    def remote(field, k, src, dst, r, c):
        return pltpu.make_async_remote_copy(
            src_ref=src, dst_ref=dst, send_sem=send_sem.at[field, k], recv_sem=recv_sem.at[field, k],
            device_id={"rows": r, "cols": c}, device_id_type=MESH,
        )

    def copies(field):
        tile = tile_ref(field)
        return dict(
            up=remote(field, 0, tile.at[0], recv_row.at[field, 1], row - 1, col),
            down=remote(field, 1, tile.at[ROWS - 1], recv_row.at[field, 0], row + 1, col),
            side=remote(field, 2, send_col.at[field], recv_col.at[field], row, other),
            up_side=remote(field, 3, send_cor.at[field, 0], recv_cor.at[field, 1], row - 1, other),
            down_side=remote(field, 4, send_cor.at[field, 1], recv_cor.at[field, 0], row + 1, other),
        )

    def send(field):
        out = copies(field)

        @pl.when(has_up)
        def _():
            out["up_side"].start()
            out["up"].start()

        @pl.when(has_down)
        def _():
            out["down_side"].start()
            out["down"].start()

        out["side"].start()

    def wait_recv(field):
        out = copies(field)
        out["side"].wait_recv()

        @pl.when(has_down)
        def _():
            out["up_side"].wait_recv()
            out["up"].wait_recv()

        @pl.when(has_up)
        def _():
            out["down_side"].wait_recv()
            out["down"].wait_recv()

    def wait_send(field):
        out = copies(field)
        out["side"].wait_send()

        @pl.when(has_up)
        def _():
            out["up_side"].wait_send()
            out["up"].wait_send()

        @pl.when(has_down)
        def _():
            out["down_side"].wait_send()
            out["down"].wait_send()

    def stage_tile(values, k, slot):
        for g in range(ROWS * SEQS):
            stage[slot, k, pl.ds((g + SEQS) * PITCH + 8, 8), :] = values[g]

    def edge_column(field, k, slot):
        start = SEQS * PITCH + 8
        last = stage[slot, k, pl.ds(start + COLS - 1, ROWS * SEQS, stride=PITCH), :]
        first = stage[slot, k, pl.ds(start, ROWS * SEQS, stride=PITCH), :]
        edge = jnp.where(first_col, last, first).astype(BF16)
        lanes = pl.ds(k * LANES, LANES)
        send_col[field, :, lanes] = edge
        send_cor[field, 0, :, lanes] = edge[:SEQS]
        send_cor[field, 1, :, lanes] = edge[-SEQS:]

    def build(field, taps, slot):
        for k in range(CHUNKS):
            lanes = pl.ds(k * LANES, LANES)
            for side, g0 in ((0, 0), (1, GROUPS - SEQS)):
                for s in range(SEQS):
                    stage[slot, k, pl.ds((g0 + s) * PITCH + 8, 8), :] = recv_row[field, side, s, :, lanes].astype(F32)
            pieces = ((recv_cor[field, 0, :, lanes], 0, SEQS), (recv_col[field, :, lanes], SEQS, ROWS * SEQS), (recv_cor[field, 1, :, lanes], GROUPS - SEQS, SEQS))
            for value, g0, count in pieces:
                value = value.astype(F32)
                stage[slot, k, pl.ds(g0 * PITCH + 7, count, stride=PITCH), :] = jnp.where(first_col, 0.0, value)
                stage[slot, k, pl.ds(g0 * PITCH + 16, count, stride=PITCH), :] = jnp.where(first_col, value, 0.0)
            for y in range(ROWS + 2):
                for d in range(3):
                    pair = [stage[slot, k, pl.ds((y * SEQS + s) * PITCH + 7 + d, 8), :] for s in range(SEQS)]
                    taps[y * 16 : (y + 1) * 16, d * CH + k * LANES : d * CH + (k + 1) * LANES] = jnp.concatenate(pair, axis=0).astype(BF16)

    def prepare(field, slot):
        tile = tile_ref(field)
        for k in range(CHUNKS):
            values = tile[:, :, :, k * LANES : (k + 1) * LANES].astype(F32).reshape(ROWS * SEQS, 8, LANES)
            stage_tile(values, k, slot)
            edge_column(field, k, slot)

    for field, group in ((0, loads[0]), (STEPS, loads[STEPS]), (1, loads[1]), (2, loads[2]), (3, loads[3])):
        for copy in group:
            copy.wait()
        prepare(field, min(field, STEPS))
        send(field)

    def conv_x(t):
        lhs = im2col(xtaps)
        for block in range(CHUNKS):
            gate_x[block] = jnp.dot(lhs, gate_columns(wx, block), preferred_element_type=F32)

    w_loads[0].wait()
    wait_recv(0)
    build(0, xtaps, 0)
    conv_x(0)
    for copy in loads[STEPS + 1]:
        copy.wait()
    w_loads[1].wait()
    wait_recv(STEPS)
    build(STEPS, htaps, STEPS)

    outs = []
    for t in range(STEPS):
        lhs = im2col(htaps)
        for block in range(CHUNKS):
            lanes = slice(block * LANES, (block + 1) * LANES)
            sums = jnp.dot(lhs, gate_columns(wh, block), preferred_element_type=F32) + gate_x[block]
            gates = [sums[:, g * LANES : (g + 1) * LANES] + bias_ref[:, g * CH + block * LANES : g * CH + (block + 1) * LANES] for g in range(4)]
            shape = (ROWS, SEQS, COLS, LANES)
            c_old = cell[:, :, :, lanes].reshape(CELLS, LANES)
            c_new = sigmoid(gates[1]) * c_old + sigmoid(gates[0]) * jnp.tanh(gates[3])
            h_new = sigmoid(gates[2]) * jnp.tanh(c_new)
            cell[:, :, :, lanes] = c_new.reshape(shape)
            hidden[t + 1, :, :, :, lanes] = h_new.reshape(shape).astype(BF16)
            if t + 1 < STEPS:
                stage_tile(h_new.reshape(ROWS * SEQS, 8, LANES), block, STEPS)
                edge_column(STEPS + t + 1, block, STEPS)
        if t + 1 < STEPS:
            send(STEPS + t + 1)
        for s in range(SEQS):
            outs.append(pltpu.make_async_copy(hidden.at[t + 1, :, s], out_hbm.at[t, s], out_sem.at[t, s]))
            outs[-1].start()
        if t + 1 < STEPS:
            wait_recv(t + 1)
            build(t + 1, xtaps, t + 1)
            conv_x(t + 1)
            wait_recv(STEPS + t + 1)
            build(STEPS + t + 1, htaps, STEPS)
    for s in range(SEQS):
        outs.append(pltpu.make_async_copy(cell.at[:, s], c_out_hbm.at[s], out_sem.at[STEPS, s]))
        outs[-1].start()
    for field in range(2 * STEPS):
        wait_send(field)
    for copy in outs:
        copy.wait()


def solution(mesh):
    row_count = mesh.shape["rows"]
    frame_spec = P(None, "batch", "rows", "cols", None)
    state_spec = P("batch", "rows", "cols", None)

    def local_run(frames, w_x, w_h, gate_bias, h_init, c_init):
        any_space = pl.BlockSpec(memory_space=pl.ANY)
        vmem = pl.BlockSpec(memory_space=pltpu.VMEM)
        fields = 2 * STEPS
        return pl.pallas_call(
            functools.partial(kernel, row_count),
            out_shape=(jax.ShapeDtypeStruct(frames.shape, BF16), jax.ShapeDtypeStruct(c_init.shape, F32)),
            in_specs=[any_space, any_space, any_space, vmem, any_space, any_space],
            out_specs=(any_space, any_space),
            scratch_shapes=[
                pltpu.VMEM((DEPTH, GATES), BF16),
                pltpu.VMEM((DEPTH, GATES), BF16),
                pltpu.VMEM((STEPS, ROWS, SEQS, COLS, CH), BF16),
                pltpu.VMEM((STEPS + 1, ROWS, SEQS, COLS, CH), BF16),
                pltpu.VMEM((ROWS, SEQS, COLS, CH), F32),
                pltpu.VMEM(((ROWS + 2) * 16, TAP_ROWS), BF16),
                pltpu.VMEM(((ROWS + 2) * 16, TAP_ROWS), BF16),
                pltpu.VMEM((CHUNKS, CELLS, 4 * LANES), F32),
                pltpu.VMEM((STEPS + 1, CHUNKS, STAGE_ROWS, LANES), F32),
                pltpu.VMEM((fields, ROWS * SEQS, CH), BF16),
                pltpu.VMEM((fields, 2, SEQS, CH), BF16),
                pltpu.VMEM((fields, 2, SEQS, COLS, CH), BF16),
                pltpu.VMEM((fields, ROWS * SEQS, CH), BF16),
                pltpu.VMEM((fields, 2, SEQS, CH), BF16),
                pltpu.SemaphoreType.DMA((STEPS + 2, SEQS)),
                pltpu.SemaphoreType.DMA((2,)),
                pltpu.SemaphoreType.DMA((STEPS + 1, SEQS)),
                pltpu.SemaphoreType.DMA((fields, 5)),
                pltpu.SemaphoreType.DMA((fields, 5)),
            ],
            compiler_params=pltpu.CompilerParams(collective_id=0, has_side_effects=True, vmem_limit_bytes=62 * 2**20),
        )(frames, w_x.reshape(DEPTH, GATES), w_h.reshape(DEPTH, GATES), gate_bias.reshape(1, GATES), h_init, c_init)

    return jax.shard_map(local_run, mesh=mesh, in_specs=(frame_spec, P(), P(), P(), state_spec, state_spec), out_specs=(frame_spec, state_spec), check_vma=False)
```

time: 148 us -> 39.9 us (0.27)
  matrix products: 56.3 us -> 0 us
  starting transfers between devices: 37.5 us -> 0 us
  waiting for transfers between devices: 36.5 us -> 0 us
  Pallas kernels: 0 us -> 33.8 us
  other arithmetic: 9.83 us -> 0 us
    dot_general x8 -> x0, matrix products: 56.3 us -> none  [conv_taps(): jnp.dot(flat_patches, flat_weights, preferred_element_type=jnp.float32)]
    ppermute x20 -> x0, starting transfers between devices: 37.5 us -> none  [the longest x10 24.6 us: edge_swap(): from_prev = lax.ppermute(high_edge, axis_label, down_pairs)]
    ppermute x20 -> x0, waiting for transfers between devices: 36.5 us -> none  [the longest x10 33.9 us: edge_swap(): from_next = lax.ppermute(low_edge, axis_label, up_pairs)]
    pallas_call x0 -> x1, Pallas kernels: none -> 33.8 us  [local_run(): pl.pallas_call(functools.partial(kernel, row_count), out_shape=(jax.Shape...]
    dynamic_update_slice x4 -> x0, other arithmetic: 4.45 us -> none  [local_run(): final_pair, all_hidden = lax.scan(step_fn, (h_init, c_init), frames_ext)]
    unnamed x12 -> x2, local copies, waits for them, and re-layouts: 0.92 us -> 3.86 us
    while x28 -> x0, other arithmetic: 2.7 us -> none
    concatenate x5 -> x0, other arithmetic: 2.69 us -> none  [the longest x1 2.12 us: edge_swap(): return jnp.concatenate([from_prev, tile_arr, from_next], axis=split_dim)]
  transfers between devices with their start and end apart: 20 -> 0, of which waited for: 11 -> 0; matrix products, arithmetic and copies ran while one was open for 25% -> 0% of each run, Pallas kernels for 0% -> 0%
where the time goes in v1:
time: 39.9 us; the launch traced here: 39.6 us
  Pallas kernels  33.8 us (85%)
  local copies, waits for them, and re-layouts  5.15 us (13%)
  between operations  0.64 us (2%)
    pallas_call x1, Pallas kernels, local_run(): pl.pallas_call(functools.partial(kernel, row_count), out_shape=(jax.Shape...  33.8 us
    unnamed x2, local copies, waits for them, and re-layouts  3.86 us
    reshape x1, local copies, waits for them, and re-layouts, local_run(): gate_bias.reshape(1, GATES)  1.3 us

profile of v1, /device:TPU:0, one launch (start us, length us, event | category | flops | bytes accessed | tf_op | source)
XLA Modules:
  0.0 39.6 jit_solution(14541911551919883705)
XLA Ops:
  0.6 1.3 %reshape.15.bias_ref = f32[1,1536]{1,0:T(1,128)} reshape(f32[1536]{0:T(1024)} %param.9) | data formatting | bytes 12288 | tf_op jit(solution)/shard_map/reshape | solution.py:293
  1.9 33.8 %shard_map.77 = (bf16[4,2,16,8,384]{4,3,2,1,0:T(8,128)(2,1)}, f32[2,16,8,384]{3,2,1,0:T(8,128)}) custom-call(bf16[4,2,16,8,384]{4,3,2,1,0:T(8,128)(2,1)} %frames_hbm.1, bf16[3456,1536]{1,0:T(8,128)(2,1)} %bitcast.2, bf16[3456,1536]{1,0:T(8,128)(2,1)} %bitcast.3, f32[1,1536]{1,0:T(1,128)} %reshape.15.bias_ref, bf16[2,16,8,384]{3,2,1,0:T(8,128)(2,1)} %h_hbm.1, ...), custom_call_target="tpu_custom_call" | custom-call | tf_op jit(solution)/shard_map/pallas_call | solution.py:266
  35.7 2.1 %copy.10 = bf16[4,2,16,8,384]{4,3,2,1,0:T(8,128)(2,1)} copy(bf16[4,2,16,8,384]{4,3,2,1,0:T(8,128)(2,1)} %get-tuple-element.4) | data formatting | bytes 1572864
  37.8 1.8 %copy.11 = f32[2,16,8,384]{3,2,1,0:T(8,128)} copy(f32[2,16,8,384]{3,2,1,0:T(8,128)} %get-tuple-element.5) | data formatting | bytes 786432

commit v2 on v1

v2 whole, which is shorter than its diff:
```python
import functools

import jax
import jax.numpy as jnp
from jax import lax
from jax.experimental import pallas as pl
from jax.experimental.pallas import tpu as pltpu
from jax.sharding import PartitionSpec as P

MESH = pl.DeviceIdType.MESH
BF16 = jnp.bfloat16
F32 = jnp.float32

STEPS = 4
SEQS = 2
ROWS = 16
COLS = 8
CH = 384
LANES = 128
CHUNKS = CH // LANES
TAP_ROWS = 3 * CH
DEPTH = 3 * TAP_ROWS
GATES = 4 * CH
CELLS = ROWS * SEQS * COLS
PITCH = 16
GROUPS = (ROWS + 2) * SEQS
STAGE_ROWS = GROUPS * PITCH + 8
CENTER = 4


def sigmoid(value):
    return 0.5 * jnp.tanh(0.5 * value) + 0.5


def halves(source, taps):
    return [(source, tap, k) for tap in taps for k in range(CHUNKS)]


def kernel(
    row_count,
    frames_hbm, wx_hbm, wh_hbm, bias_hbm, h_hbm, c_hbm,
    hidden_out, cell,
    wx, wh, bias, frames, h_start, xtaps, htaps, gates, stage,
    send_col, send_cor, recv_row, recv_col, recv_cor,
    in_sem, w_sem, send_sem, recv_sem,
):
    row = lax.axis_index("rows")
    col = lax.axis_index("cols")
    other = 1 - col
    has_up = row > 0
    has_down = row < row_count - 1
    first_col = col == 0

    frame_loads = [[pltpu.make_async_copy(frames_hbm.at[t, s], frames.at[t, :, s], in_sem.at[t, s]) for s in range(SEQS)] for t in range(STEPS)]
    h_loads = [pltpu.make_async_copy(h_hbm.at[s], h_start.at[:, s], in_sem.at[STEPS, s]) for s in range(SEQS)]
    c_loads = [pltpu.make_async_copy(c_hbm.at[s], cell.at[:, s], in_sem.at[STEPS + 1, s]) for s in range(SEQS)]
    bias_load = pltpu.make_async_copy(bias_hbm, bias, w_sem.at[0, 3])
    spans = (pl.ds(CENTER * CH, CH), pl.ds(0, CENTER * CH), pl.ds((CENTER + 1) * CH, DEPTH - (CENTER + 1) * CH))
    x_loads, w_loads = [[pltpu.make_async_copy(src.at[span], dst.at[span], w_sem.at[i, n]) for n, span in enumerate(spans)] for i, (src, dst) in enumerate(((wx_hbm, wx), (wh_hbm, wh)))]
    for copy in (*frame_loads[0], *h_loads, x_loads[0], w_loads[0], *frame_loads[1], *frame_loads[2], *frame_loads[3], *x_loads[1:], *c_loads, bias_load, *w_loads[1:]):
        copy.start()

    recv_row[...] = jnp.zeros_like(recv_row)
    recv_cor[...] = jnp.zeros_like(recv_cor)

    barrier = pltpu.get_barrier_semaphore()

    def greet(r, c):
        pl.semaphore_signal(barrier, inc=1, device_id={"rows": r, "cols": c}, device_id_type=MESH)

    greet(row, other)

    @pl.when(has_up)
    def _():
        greet(row - 1, col)
        greet(row - 1, other)

    @pl.when(has_down)
    def _():
        greet(row + 1, col)
        greet(row + 1, other)

    def greeted():
        inner = jnp.logical_and(has_up, has_down)

        @pl.when(inner)
        def _():
            pl.semaphore_wait(barrier, 5)

        @pl.when(jnp.logical_not(inner))
        def _():
            pl.semaphore_wait(barrier, 3)

    def tile_ref(field):
        if field < STEPS:
            return frames.at[field]
        return h_start if field == STEPS else hidden_out.at[field - STEPS - 1]

    def remote(field, k, src, dst, r, c):
        return pltpu.make_async_remote_copy(
            src_ref=src, dst_ref=dst, send_sem=send_sem.at[field, k], recv_sem=recv_sem.at[field, k],
            device_id={"rows": r, "cols": c}, device_id_type=MESH,
        )

    def copies(field):
        tile = tile_ref(field)
        return dict(
            up=remote(field, 0, tile.at[0], recv_row.at[field, 1], row - 1, col),
            down=remote(field, 1, tile.at[ROWS - 1], recv_row.at[field, 0], row + 1, col),
            side=remote(field, 2, send_col.at[field], recv_col.at[field], row, other),
            up_side=remote(field, 3, send_cor.at[field, 0], recv_cor.at[field, 1], row - 1, other),
            down_side=remote(field, 4, send_cor.at[field, 1], recv_cor.at[field, 0], row + 1, other),
        )

    def send(field):
        out = copies(field)

        @pl.when(has_up)
        def _():
            out["up_side"].start()
            out["up"].start()

        @pl.when(has_down)
        def _():
            out["down_side"].start()
            out["down"].start()

        out["side"].start()

    def wait_recv(field):
        out = copies(field)
        out["side"].wait_recv()

        @pl.when(has_down)
        def _():
            out["up_side"].wait_recv()
            out["up"].wait_recv()

        @pl.when(has_up)
        def _():
            out["down_side"].wait_recv()
            out["down"].wait_recv()

    def wait_send(field):
        out = copies(field)
        out["side"].wait_send()

        @pl.when(has_up)
        def _():
            out["up_side"].wait_send()
            out["up"].wait_send()

        @pl.when(has_down)
        def _():
            out["down_side"].wait_send()
            out["down"].wait_send()

    def shift_lanes(d, k):
        return slice(d * CH + k * LANES, d * CH + (k + 1) * LANES)

    def field_taps(field):
        return xtaps if field < STEPS else htaps.at[field % 2]

    def own_tile(field, values, k, taps, slot):
        for g in range(ROWS * SEQS):
            stage[slot, k, pl.ds((g + SEQS) * PITCH + 8, 8), :] = values[g]
        if taps is not None:
            taps[16 : 16 + CELLS, shift_lanes(1, k)] = values.reshape(CELLS, LANES).astype(BF16)
        start = SEQS * PITCH + 8
        last = stage[slot, k, pl.ds(start + COLS - 1, ROWS * SEQS, stride=PITCH), :]
        first = stage[slot, k, pl.ds(start, ROWS * SEQS, stride=PITCH), :]
        edge = jnp.where(first_col, last, first).astype(BF16)
        lanes = pl.ds(k * LANES, LANES)
        send_col[field, :, lanes] = edge
        send_cor[field, 0, :, lanes] = edge[:SEQS]
        send_cor[field, 1, :, lanes] = edge[-SEQS:]

    def prepare(field, taps, slot):
        tile = tile_ref(field)
        for k in range(CHUNKS):
            values = tile[:, :, :, k * LANES : (k + 1) * LANES].astype(F32).reshape(ROWS * SEQS, 8, LANES)
            own_tile(field, values, k, taps, slot)

    def build(field, taps, slot, own_done):
        for k in range(CHUNKS):
            lanes = pl.ds(k * LANES, LANES)
            for side, g0 in ((0, 0), (1, GROUPS - SEQS)):
                for s in range(SEQS):
                    stage[slot, k, pl.ds((g0 + s) * PITCH + 8, 8), :] = recv_row[field, side, s, :, lanes].astype(F32)
            pieces = ((recv_cor[field, 0, :, lanes], 0, SEQS), (recv_col[field, :, lanes], SEQS, ROWS * SEQS), (recv_cor[field, 1, :, lanes], GROUPS - SEQS, SEQS))
            for value, g0, count in pieces:
                value = value.astype(F32)
                stage[slot, k, pl.ds(g0 * PITCH + 7, count, stride=PITCH), :] = jnp.where(first_col, 0.0, value)
                stage[slot, k, pl.ds(g0 * PITCH + 16, count, stride=PITCH), :] = jnp.where(first_col, value, 0.0)
            for y in range(ROWS + 2):
                for d in range(3):
                    if own_done and d == 1 and 1 <= y <= ROWS:
                        continue
                    pair = [stage[slot, k, pl.ds((y * SEQS + s) * PITCH + 7 + d, 8), :] for s in range(SEQS)]
                    taps[y * 16 : (y + 1) * 16, shift_lanes(d, k)] = jnp.concatenate(pair, axis=0).astype(BF16)

    def operand(half, t):
        source, tap, k = half
        taps = field_taps(t if source == "x" else STEPS + t)
        dy, dx = divmod(tap, 3)
        return taps[dy * 16 : dy * 16 + CELLS, shift_lanes(dx, k)]

    def weight(half, block):
        source, tap, k = half
        w = wx if source == "x" else wh
        first = tap * CH + k * LANES
        return jnp.concatenate([w[first : first + LANES, g * CH + block * LANES : g * CH + (block + 1) * LANES] for g in range(4)], axis=1)

    def product(t, block, parts):
        lhs = jnp.concatenate([operand(p, t) for p in parts], axis=1)
        rhs = jnp.concatenate([weight(p, block) for p in parts], axis=0)
        return jnp.dot(lhs, rhs, preferred_element_type=F32)

    around = [tap for tap in range(9) if tap != CENTER]
    x_part = halves("x", around)
    h_part = halves("h", around)
    own_part = halves("x", [CENTER]) + halves("h", [CENTER])

    def cell_update(t, block):
        lanes = slice(block * LANES, (block + 1) * LANES)
        sums = product(t, block, h_part) + gates[block]
        pre = [sums[:, g * LANES : (g + 1) * LANES] + bias[pl.ds(g * CH + block * LANES, LANES)] for g in range(4)]
        shape = (ROWS, SEQS, COLS, LANES)
        c_old = cell[:, :, :, lanes].reshape(CELLS, LANES)
        c_new = sigmoid(pre[1]) * c_old + sigmoid(pre[0]) * jnp.tanh(pre[3])
        h_new = sigmoid(pre[2]) * jnp.tanh(c_new)
        cell[:, :, :, lanes] = c_new.reshape(shape)
        hidden_out[t, :, :, :, lanes] = h_new.reshape(shape).astype(BF16)
        if t + 1 < STEPS:
            own_tile(STEPS + t + 1, h_new.reshape(ROWS * SEQS, 8, LANES), block, field_taps(STEPS + t + 1), STEPS)

    for field, group in ((0, frame_loads[0]), (STEPS, h_loads)):
        for copy in group:
            copy.wait()
        prepare(field, field_taps(field), field)
    greeted()
    send(0)
    send(STEPS)
    x_loads[0].wait()
    w_loads[0].wait()
    for block in range(CHUNKS):
        gates[block] = product(0, block, own_part)
    for t in range(1, STEPS):
        for copy in frame_loads[t]:
            copy.wait()
        prepare(t, None, t)
        send(t)
    for copy in (*x_loads[1:], *c_loads, bias_load):
        copy.wait()
    wait_recv(0)
    build(0, xtaps, 0, True)
    for block in range(CHUNKS):
        gates[block] += product(0, block, x_part)
    for copy in w_loads[1:]:
        copy.wait()
    wait_recv(STEPS)
    build(STEPS, field_taps(STEPS), STEPS, True)

    for t in range(STEPS):
        for block in range(CHUNKS):
            cell_update(t, block)
        if t + 1 < STEPS:
            send(STEPS + t + 1)
            wait_recv(t + 1)
            build(t + 1, xtaps, t + 1, False)
            for block in range(CHUNKS):
                gates[block] = product(t + 1, block, x_part + own_part)
            wait_recv(STEPS + t + 1)
            build(STEPS + t + 1, field_taps(STEPS + t + 1), STEPS, True)
    for field in range(2 * STEPS):
        wait_send(field)


def write_out(hidden, cell, out_hbm, c_out_hbm, sem):
    copies = [pltpu.make_async_copy(hidden.at[t, :, s], out_hbm.at[t, s], sem.at[t, s]) for t in range(STEPS) for s in range(SEQS)]
    copies += [pltpu.make_async_copy(cell.at[:, s], c_out_hbm.at[s], sem.at[STEPS, s]) for s in range(SEQS)]
    for copy in copies:
        copy.start()
    for copy in copies:
        copy.wait()


def solution(mesh):
    row_count = mesh.shape["rows"]
    frame_spec = P(None, "batch", "rows", "cols", None)
    state_spec = P("batch", "rows", "cols", None)

    def local_run(frames, w_x, w_h, gate_bias, h_init, c_init):
        hbm = pl.BlockSpec(memory_space=pltpu.HBM)
        vmem = pl.BlockSpec(memory_space=pltpu.VMEM)
        fields = 2 * STEPS
        tile = (ROWS, SEQS, COLS, CH)

        hidden, cell = pl.pallas_call(
            functools.partial(kernel, row_count),
            out_shape=(pltpu.VMEM((STEPS,) + tile, BF16), pltpu.VMEM(tile, F32)),
            in_specs=[hbm] * 6,
            out_specs=(vmem, vmem),
            scratch_shapes=[
                pltpu.VMEM((DEPTH, GATES), BF16),
                pltpu.VMEM((DEPTH, GATES), BF16),
                pltpu.VMEM((GATES,), F32),
                pltpu.VMEM((STEPS,) + tile, BF16),
                pltpu.VMEM(tile, BF16),
                pltpu.VMEM(((ROWS + 2) * 16, TAP_ROWS), BF16),
                pltpu.VMEM((2, (ROWS + 2) * 16, TAP_ROWS), BF16),
                pltpu.VMEM((CHUNKS, CELLS, 4 * LANES), F32),
                pltpu.VMEM((STEPS + 1, CHUNKS, STAGE_ROWS, LANES), F32),
                pltpu.VMEM((fields, ROWS * SEQS, CH), BF16),
                pltpu.VMEM((fields, 2, SEQS, CH), BF16),
                pltpu.VMEM((fields, 2, SEQS, COLS, CH), BF16),
                pltpu.VMEM((fields, ROWS * SEQS, CH), BF16),
                pltpu.VMEM((fields, 2, SEQS, CH), BF16),
                pltpu.SemaphoreType.DMA((STEPS + 2, SEQS)),
                pltpu.SemaphoreType.DMA((2, 4)),
                pltpu.SemaphoreType.DMA((fields, 5)),
                pltpu.SemaphoreType.DMA((fields, 5)),
            ],
            compiler_params=pltpu.CompilerParams(collective_id=0, has_side_effects=True, vmem_limit_bytes=48 * 2**20),
        )(*(pltpu.with_memory_space_constraint(a, pltpu.HBM) for a in (frames, w_x.reshape(DEPTH, GATES), w_h.reshape(DEPTH, GATES), gate_bias, h_init, c_init)))
        return pl.pallas_call(
            write_out,
            out_shape=(jax.ShapeDtypeStruct(frames.shape, BF16), jax.ShapeDtypeStruct(c_init.shape, F32)),
            in_specs=[vmem, vmem],
            out_specs=(hbm, hbm),
            scratch_shapes=[pltpu.SemaphoreType.DMA((STEPS + 1, SEQS))],
        )(*(pltpu.with_memory_space_constraint(a, pltpu.VMEM) for a in (hidden, cell)))

    return jax.shard_map(local_run, mesh=mesh, in_specs=(frame_spec, P(), P(), P(), state_spec, state_spec), out_specs=(frame_spec, state_spec), check_vma=False)
```

time: 39.9 us -> 34.3 us (0.86)
  local copies, waits for them, and re-layouts: 5.15 us -> 0 us
  Pallas kernels: 33.8 us -> 33.4 us
    unnamed x2 -> x0, local copies, waits for them, and re-layouts: 3.86 us -> none
    reshape x1 -> x0, local copies, waits for them, and re-layouts: 1.3 us -> none  [local_run(): gate_bias.reshape(1, GATES)]
    pallas_call x1 -> x2, Pallas kernels: 33.8 us -> 33.4 us  [the longest x1 32.3 us: local_run(): pl.pallas_call(functools.partial(kernel, row_count), out_shape=(pltpu.VME...]
where the time goes in v2:
time: 34.3 us; the launch traced here: 34.2 us
  Pallas kernels  33.4 us (97%)
  between operations  0.8 us (2%)
    pallas_call x1, Pallas kernels, local_run(): pl.pallas_call(functools.partial(kernel, row_count), out_shape=(pltpu.VME...  32.3 us
    pallas_call x1, Pallas kernels, local_run(): pl.pallas_call(write_out, out_shape=(jax.ShapeDtypeStruct(frames.shape, B...  1.09 us

profile of v2, /device:TPU:0, one launch (start us, length us, event | category | flops | bytes accessed | tf_op | source)
XLA Modules:
  0.0 34.2 jit_solution(18101718270016298314)
XLA Ops:
  0.6 32.3 %shard_map.77 = (bf16[4,16,2,8,384]{4,3,2,1,0:T(8,128)(2,1)S(1)}, f32[16,2,8,384]{3,2,1,0:T(8,128)S(1)}) custom-call(bf16[4,2,16,8,384]{4,3,2,1,0:T(8,128)(2,1)} %frames_hbm.1, bf16[3456,1536]{1,0:T(8,128)(2,1)} %bitcast.2, bf16[3456,1536]{1,0:T(8,128)(2,1)} %bitcast.3, f32[1536]{0:T(1024)} %bias_hbm.1, bf16[2,16,8,384]{3,2,1,0:T(8,128)(2,1)} %h_hbm.1, ...), custom_call_target="tpu_custom_call" | custom-call | tf_op jit(solution)/shard_map/pallas_call | solution.py:299
  32.9 1.1 %shard_map.78 = (bf16[4,2,16,8,384]{4,3,2,1,0:T(8,128)(2,1)}, f32[2,16,8,384]{3,2,1,0:T(8,128)}) custom-call(bf16[4,16,2,8,384]{4,3,2,1,0:T(8,128)(2,1)S(1)} %get-tuple-element.4.hidden, f32[16,2,8,384]{3,2,1,0:T(8,128)S(1)} %get-tuple-element.5.cell), custom_call_target="tpu_custom_call" | custom-call | tf_op jit(solution)/shard_map/pallas_call | solution.py:326

commit v3 on v2

v3 whole, which is shorter than its diff:
```python
import functools

import jax
import jax.numpy as jnp
from jax import lax
from jax.experimental import pallas as pl
from jax.experimental.pallas import tpu as pltpu
from jax.sharding import PartitionSpec as P

MESH = pl.DeviceIdType.MESH
BF16 = jnp.bfloat16
F32 = jnp.float32

STEPS = 4
SEQS = 2
ROWS = 16
COLS = 8
CH = 384
LANES = 128
CHUNKS = CH // LANES
TAP_ROWS = 3 * CH
DEPTH = 3 * TAP_ROWS
GATES = 4 * CH
CELLS = ROWS * SEQS * COLS
PITCH = 16
GROUPS = (ROWS + 2) * SEQS
STAGE_ROWS = GROUPS * PITCH + 8
OWN = (4,)
VERTICAL = (1, 7)
SIDE = (0, 2, 3, 5, 6, 8)


def sigmoid(value):
    return 0.5 * jnp.tanh(0.5 * value) + 0.5


def halves(source, taps):
    return [(source, tap, k) for tap in taps for k in range(CHUNKS)]


def kernel(
    row_count,
    frames_hbm, wx_hbm, wh_hbm, bias_hbm, h_hbm, c_hbm,
    hidden_out, cell,
    wx, wh, bias, frames, h_start, xtaps, htaps, gates, stage,
    send_col, send_cor, recv_row, recv_col, recv_cor,
    load_sem, send_sem, recv_sem,
):
    row = lax.axis_index("rows")
    col = lax.axis_index("cols")
    other = 1 - col
    has_up = row > 0
    has_down = row < row_count - 1
    inner = jnp.logical_and(has_up, has_down)
    first_col = col == 0

    group_of = {}
    for name in ("frame0", "state", "own_x", "own_h", "frame1", "frames", "cell", "bias", "near_x", "far_x", "last_x", "most_h", "last_h"):
        group_of[name] = load_sem.at[len(group_of)]

    def load(name, queue, pairs):
        for src, dst in pairs:
            pltpu.make_async_copy(src, dst, group_of[name]).start(priority=queue)

    def loaded(name, whole):
        pltpu.make_async_copy(whole, whole, group_of[name]).wait()

    def frame_pairs(times):
        return [(frames_hbm.at[t, s], frames.at[t, :, s]) for t in times for s in range(SEQS)]

    def tap_pairs(src, dst, taps):
        return [(src.at[pl.ds(tap * CH, CH)], dst.at[pl.ds(tap * CH, CH)]) for tap in taps]

    def taps_like(dst, count):
        return dst.at[pl.ds(0, count * CH)]

    load("frame0", 0, frame_pairs([0]))
    load("state", 0, [(h_hbm.at[s], h_start.at[:, s]) for s in range(SEQS)])
    load("own_x", 1, tap_pairs(wx_hbm, wx, OWN))
    load("own_h", 1, tap_pairs(wh_hbm, wh, OWN))
    load("frame1", 0, frame_pairs([1]))
    load("frames", 0, frame_pairs([2, 3]))
    load("cell", 0, [(c_hbm.at[s], cell.at[:, s]) for s in range(SEQS)])
    load("bias", 0, [(bias_hbm, bias)])
    load("near_x", 1, tap_pairs(wx_hbm, wx, VERTICAL))
    load("far_x", 1, tap_pairs(wx_hbm, wx, SIDE[:4]))
    load("last_x", 1, tap_pairs(wx_hbm, wx, SIDE[4:]))
    load("most_h", 1, tap_pairs(wh_hbm, wh, VERTICAL + SIDE[:4]))
    load("last_h", 1, tap_pairs(wh_hbm, wh, SIDE[4:]))

    recv_row[...] = jnp.zeros_like(recv_row)
    recv_cor[...] = jnp.zeros_like(recv_cor)

    barrier = pltpu.get_barrier_semaphore()

    def greet(r, c):
        pl.semaphore_signal(barrier, inc=1, device_id={"rows": r, "cols": c}, device_id_type=MESH)

    greet(row, other)

    @pl.when(has_up)
    def _():
        greet(row - 1, col)
        greet(row - 1, other)

    @pl.when(has_down)
    def _():
        greet(row + 1, col)
        greet(row + 1, other)

    def greeted():
        @pl.when(inner)
        def _():
            pl.semaphore_wait(barrier, 5)

        @pl.when(jnp.logical_not(inner))
        def _():
            pl.semaphore_wait(barrier, 3)

    def tile_ref(field):
        if field < STEPS:
            return frames.at[field]
        return h_start if field == STEPS else hidden_out.at[field - STEPS - 1]

    def field_taps(field):
        return xtaps.at[field % 2] if field < STEPS else htaps.at[field % 2]

    def remote(field, n, src, dst, r, c):
        return pltpu.make_async_remote_copy(
            src_ref=src, dst_ref=dst, send_sem=send_sem.at[n], recv_sem=recv_sem.at[field, (0, 0, 1, 2, 2)[n]],
            device_id={"rows": r, "cols": c}, device_id_type=MESH,
        )

    def copies(field):
        tile = tile_ref(field)
        return dict(
            up=remote(field, 0, tile.at[0], recv_row.at[field, 1], row - 1, col),
            down=remote(field, 1, tile.at[ROWS - 1], recv_row.at[field, 0], row + 1, col),
            side=remote(field, 2, send_col.at[field], recv_col.at[field], row, other),
            up_side=remote(field, 3, send_cor.at[field, 0], recv_cor.at[field, 1], row - 1, other),
            down_side=remote(field, 4, send_cor.at[field, 1], recv_cor.at[field, 0], row + 1, other),
        )

    def send(field):
        out = copies(field)

        @pl.when(has_up)
        def _():
            out["up_side"].start()
            out["up"].start()

        @pl.when(has_down)
        def _():
            out["down_side"].start()
            out["down"].start()

        out["side"].start()

    def pair_arrived(field, n, both):
        @pl.when(inner)
        def _():
            pltpu.make_async_copy(both, both, recv_sem.at[field, n]).wait()

        @pl.when(jnp.logical_not(inner))
        def _():
            pltpu.make_async_copy(both.at[0], both.at[0], recv_sem.at[field, n]).wait()

    def rows_arrived(field):
        pair_arrived(field, 0, recv_row.at[field])

    def sides_arrived(field):
        pltpu.make_async_copy(recv_col.at[field], recv_col.at[field], recv_sem.at[field, 1]).wait()
        pair_arrived(field, 2, recv_cor.at[field])

    def all_sent():
        whole_row, whole_cor = recv_row.at[:, 0], recv_cor.at[:, 0]
        remote(0, 2, recv_col, recv_col, row, other).wait_send()

        @pl.when(has_up)
        def _():
            remote(0, 0, whole_row, whole_row, row - 1, col).wait_send()
            remote(0, 3, whole_cor, whole_cor, row - 1, other).wait_send()

        @pl.when(has_down)
        def _():
            remote(0, 1, whole_row, whole_row, row + 1, col).wait_send()
            remote(0, 4, whole_cor, whole_cor, row + 1, other).wait_send()

    def shift_lanes(d, k):
        return slice(d * CH + k * LANES, d * CH + (k + 1) * LANES)

    def slot_of(field):
        return min(field, STEPS)

    def own_tile(field, values, k):
        slot = slot_of(field)
        for g in range(ROWS * SEQS):
            stage[slot, k, pl.ds((g + SEQS) * PITCH + 8, 8), :] = values[g]
        if field == 0 or field >= STEPS:
            field_taps(field)[16 : 16 + CELLS, shift_lanes(1, k)] = values.reshape(CELLS, LANES).astype(BF16)
        begin = SEQS * PITCH + 8
        last = stage[slot, k, pl.ds(begin + COLS - 1, ROWS * SEQS, stride=PITCH), :]
        first = stage[slot, k, pl.ds(begin, ROWS * SEQS, stride=PITCH), :]
        edge = jnp.where(first_col, last, first).astype(BF16)
        lanes = pl.ds(k * LANES, LANES)
        send_col[field, :, lanes] = edge
        send_cor[field, 0, :, lanes] = edge[:SEQS]
        send_cor[field, 1, :, lanes] = edge[-SEQS:]

    def prepare(field):
        tile = tile_ref(field)
        for k in range(CHUNKS):
            values = tile[:, :, :, k * LANES : (k + 1) * LANES].astype(F32).reshape(ROWS * SEQS, 8, LANES)
            own_tile(field, values, k)

    def shifted(field, y, d, k):
        slot = slot_of(field)
        pair = [stage[slot, k, pl.ds((y * SEQS + s) * PITCH + 7 + d, 8), :] for s in range(SEQS)]
        field_taps(field)[y * 16 : (y + 1) * 16, shift_lanes(d, k)] = jnp.concatenate(pair, axis=0).astype(BF16)

    def build_rows(field):
        slot = slot_of(field)
        for k in range(CHUNKS):
            lanes = pl.ds(k * LANES, LANES)
            for side, g0 in ((0, 0), (1, GROUPS - SEQS)):
                for s in range(SEQS):
                    stage[slot, k, pl.ds((g0 + s) * PITCH + 8, 8), :] = recv_row[field, side, s, :, lanes].astype(F32)
            for y in (0, ROWS + 1) if field == 0 or field >= STEPS else range(ROWS + 2):
                shifted(field, y, 1, k)

    def build_sides(field):
        slot = slot_of(field)
        for k in range(CHUNKS):
            lanes = pl.ds(k * LANES, LANES)
            pieces = ((recv_cor[field, 0, :, lanes], 0, SEQS), (recv_col[field, :, lanes], SEQS, ROWS * SEQS), (recv_cor[field, 1, :, lanes], GROUPS - SEQS, SEQS))
            for value, g0, count in pieces:
                value = value.astype(F32)
                stage[slot, k, pl.ds(g0 * PITCH + 7, count, stride=PITCH), :] = jnp.where(first_col, 0.0, value)
                stage[slot, k, pl.ds(g0 * PITCH + 16, count, stride=PITCH), :] = jnp.where(first_col, value, 0.0)
            for y in range(ROWS + 2):
                shifted(field, y, 0, k)
                shifted(field, y, 2, k)

    def operand(half, t):
        source, tap, k = half
        taps = field_taps(t if source == "x" else STEPS + t)
        dy, dx = divmod(tap, 3)
        return taps[dy * 16 : dy * 16 + CELLS, shift_lanes(dx, k)]

    def weight(half, block):
        source, tap, k = half
        w = wx if source == "x" else wh
        first = tap * CH + k * LANES
        return jnp.concatenate([w[first : first + LANES, g * CH + block * LANES : g * CH + (block + 1) * LANES] for g in range(4)], axis=1)

    def product(t, block, parts):
        lhs = jnp.concatenate([operand(p, t) for p in parts], axis=1)
        rhs = jnp.concatenate([weight(p, block) for p in parts], axis=0)
        return jnp.dot(lhs, rhs, preferred_element_type=F32)

    def cell_update(t, block, sums):
        lanes = slice(block * LANES, (block + 1) * LANES)
        pre = [sums[:, g * LANES : (g + 1) * LANES] + bias[pl.ds(g * CH + block * LANES, LANES)] for g in range(4)]
        shape = (ROWS, SEQS, COLS, LANES)
        c_old = cell[:, :, :, lanes].reshape(CELLS, LANES)
        c_new = sigmoid(pre[1]) * c_old + sigmoid(pre[0]) * jnp.tanh(pre[3])
        h_new = sigmoid(pre[2]) * jnp.tanh(c_new)
        cell[:, :, :, lanes] = c_new.reshape(shape)
        hidden_out[t, :, :, :, lanes] = h_new.reshape(shape).astype(BF16)
        if t + 1 < STEPS:
            own_tile(STEPS + t + 1, h_new.reshape(ROWS * SEQS, 8, LANES), block)

    x_all = halves("x", VERTICAL + SIDE)
    x_own, x_vertical, x_side = (halves("x", taps) for taps in (OWN, VERTICAL, SIDE))
    h_own, h_vertical, h_side = (halves("h", taps) for taps in (OWN, VERTICAL, SIDE))

    def add(t, block, parts):
        gates[t, block] += product(t, block, parts)

    loaded("frame0", frames.at[0])
    prepare(0)
    loaded("state", h_start)
    prepare(STEPS)
    greeted()
    send(0)
    send(STEPS)
    loaded("own_x", taps_like(wx, 1))
    loaded("own_h", taps_like(wh, 1))
    loaded("frame1", frames.at[1])
    for block in range(CHUNKS):
        gates[0, block] = product(0, block, x_own + h_own)
    prepare(1)
    send(1)
    loaded("near_x", taps_like(wx, 2))
    rows_arrived(0)
    build_rows(0)
    for block in range(CHUNKS):
        add(0, block, x_vertical)
    loaded("far_x", taps_like(wx, 4))
    sides_arrived(0)
    build_sides(0)
    for block in range(CHUNKS):
        add(0, block, x_side[:12])
    loaded("last_x", taps_like(wx, 2))
    for block in range(CHUNKS):
        add(0, block, x_side[12:])
    loaded("frames", frames.at[pl.ds(2, 2)])
    rows_arrived(1)
    sides_arrived(1)
    build_rows(1)
    build_sides(1)
    for block in range(CHUNKS):
        gates[1, block] = product(1, block, x_all[:16])
    prepare(2)
    prepare(3)
    send(2)
    send(3)
    loaded("cell", cell)
    loaded("bias", bias)
    loaded("most_h", taps_like(wh, 6))
    rows_arrived(STEPS)
    sides_arrived(STEPS)
    build_rows(STEPS)
    build_sides(STEPS)
    for block in range(CHUNKS):
        add(0, block, h_vertical + h_side[:12])
    loaded("last_h", taps_like(wh, 2))
    for block in range(CHUNKS):
        cell_update(0, block, gates[0, block] + product(0, block, h_side[12:]))
    send(STEPS + 1)

    rest = {1: x_all[16:], 2: x_all[12:], 3: x_all[6:]}
    ahead = {1: x_all[:12], 2: x_all[:6]}
    for t in range(1, STEPS):
        if t in ahead:
            rows_arrived(t + 1)
            sides_arrived(t + 1)
            build_rows(t + 1)
            build_sides(t + 1)
            for block in range(CHUNKS):
                gates[t + 1, block] = product(t + 1, block, ahead[t])
        for block in range(CHUNKS):
            add(t, block, rest[t] + x_own + h_own)
        rows_arrived(STEPS + t)
        build_rows(STEPS + t)
        for block in range(CHUNKS):
            add(t, block, h_vertical)
        sides_arrived(STEPS + t)
        if t + 1 == STEPS:
            all_sent()
        build_sides(STEPS + t)
        for block in range(CHUNKS):
            cell_update(t, block, gates[t, block] + product(t, block, h_side))
        if t + 1 < STEPS:
            send(STEPS + t + 1)


def write_out(hidden, cell, out_hbm, c_out_hbm, sem):
    copies = [pltpu.make_async_copy(hidden.at[t, :, s], out_hbm.at[t, s], sem.at[t, s]) for t in range(STEPS) for s in range(SEQS)]
    copies += [pltpu.make_async_copy(cell.at[:, s], c_out_hbm.at[s], sem.at[STEPS, s]) for s in range(SEQS)]
    for copy in copies:
        copy.start()
    for copy in copies:
        copy.wait()


def solution(mesh):
    row_count = mesh.shape["rows"]
    frame_spec = P(None, "batch", "rows", "cols", None)
    state_spec = P("batch", "rows", "cols", None)

    def local_run(frames, w_x, w_h, gate_bias, h_init, c_init):
        hbm = pl.BlockSpec(memory_space=pltpu.HBM)
        vmem = pl.BlockSpec(memory_space=pltpu.VMEM)
        fields = 2 * STEPS
        tile = (ROWS, SEQS, COLS, CH)

        hidden, cell = pl.pallas_call(
            functools.partial(kernel, row_count),
            out_shape=(pltpu.VMEM((STEPS,) + tile, BF16), pltpu.VMEM(tile, F32)),
            in_specs=[hbm] * 6,
            out_specs=(vmem, vmem),
            scratch_shapes=[
                pltpu.VMEM((DEPTH, GATES), BF16),
                pltpu.VMEM((DEPTH, GATES), BF16),
                pltpu.VMEM((GATES,), F32),
                pltpu.VMEM((STEPS,) + tile, BF16),
                pltpu.VMEM(tile, BF16),
                pltpu.VMEM((2, (ROWS + 2) * 16, TAP_ROWS), BF16),
                pltpu.VMEM((2, (ROWS + 2) * 16, TAP_ROWS), BF16),
                pltpu.VMEM((STEPS, CHUNKS, CELLS, 4 * LANES), F32),
                pltpu.VMEM((STEPS + 1, CHUNKS, STAGE_ROWS, LANES), F32),
                pltpu.VMEM((fields, ROWS * SEQS, CH), BF16),
                pltpu.VMEM((fields, 2, SEQS, CH), BF16),
                pltpu.VMEM((fields, 2, SEQS, COLS, CH), BF16),
                pltpu.VMEM((fields, ROWS * SEQS, CH), BF16),
                pltpu.VMEM((fields, 2, SEQS, CH), BF16),
                pltpu.SemaphoreType.DMA((13,)),
                pltpu.SemaphoreType.DMA((5,)),
                pltpu.SemaphoreType.DMA((fields, 3)),
            ],
            compiler_params=pltpu.CompilerParams(collective_id=0, has_side_effects=True, vmem_limit_bytes=48 * 2**20),
        )(*(pltpu.with_memory_space_constraint(a, pltpu.HBM) for a in (frames, w_x.reshape(DEPTH, GATES), w_h.reshape(DEPTH, GATES), gate_bias, h_init, c_init)))
        return pl.pallas_call(
            write_out,
            out_shape=(jax.ShapeDtypeStruct(frames.shape, BF16), jax.ShapeDtypeStruct(c_init.shape, F32)),
            in_specs=[vmem, vmem],
            out_specs=(hbm, hbm),
            scratch_shapes=[pltpu.SemaphoreType.DMA((STEPS + 1, SEQS))],
        )(*(pltpu.with_memory_space_constraint(a, pltpu.VMEM) for a in (hidden, cell)))

    return jax.shard_map(local_run, mesh=mesh, in_specs=(frame_spec, P(), P(), P(), state_spec, state_spec), out_specs=(frame_spec, state_spec), check_vma=False)
```

time: 34.3 us -> 32.3 us (0.942)
  Pallas kernels: 33.4 us -> 31.4 us
    pallas_call x1, Pallas kernels: 32.3 us -> 30.3 us  [local_run(): pl.pallas_call(functools.partial(kernel, row_count), out_shape=(pltpu.VME...]
where the time goes in v3:
time: 32.3 us; the launch traced here: 32.2 us
  Pallas kernels  31.4 us (97%)
  between operations  0.8 us (2%)
    pallas_call x1, Pallas kernels, local_run(): pl.pallas_call(functools.partial(kernel, row_count), out_shape=(pltpu.VME...  30.3 us
    pallas_call x1, Pallas kernels, local_run(): pl.pallas_call(write_out, out_shape=(jax.ShapeDtypeStruct(frames.shape, B...  1.09 us

profile of v3, /device:TPU:0, one launch (start us, length us, event | category | flops | bytes accessed | tf_op | source)
XLA Modules:
  0.0 32.2 jit_solution(6160581233411157710)
XLA Ops:
  0.6 30.3 %shard_map.77 = (bf16[4,16,2,8,384]{4,3,2,1,0:T(8,128)(2,1)S(1)}, f32[16,2,8,384]{3,2,1,0:T(8,128)S(1)}) custom-call(bf16[4,2,16,8,384]{4,3,2,1,0:T(8,128)(2,1)} %frames_hbm.1, bf16[3456,1536]{1,0:T(8,128)(2,1)} %bitcast.2, bf16[3456,1536]{1,0:T(8,128)(2,1)} %bitcast.3, f32[1536]{0:T(1024)} %bias_hbm.1, bf16[2,16,8,384]{3,2,1,0:T(8,128)(2,1)} %h_hbm.1, ...), custom_call_target="tpu_custom_call" | custom-call | tf_op jit(solution)/shard_map/pallas_call | solution.py:378
  31.0 1.1 %shard_map.78 = (bf16[4,2,16,8,384]{4,3,2,1,0:T(8,128)(2,1)}, f32[2,16,8,384]{3,2,1,0:T(8,128)}) custom-call(bf16[4,16,2,8,384]{4,3,2,1,0:T(8,128)(2,1)S(1)} %get-tuple-element.4.hidden, f32[16,2,8,384]{3,2,1,0:T(8,128)S(1)} %get-tuple-element.5.cell), custom_call_target="tpu_custom_call" | custom-call | tf_op jit(solution)/shard_map/pallas_call | solution.py:404

commit v4 on v3

--- a/solution.py
+++ b/solution.py
@@ -123,7 +123,7 @@
         return h_start if field == STEPS else hidden_out.at[field - STEPS - 1]
 
     def field_taps(field):
-        return xtaps.at[field % 2] if field < STEPS else htaps.at[field % 2]
+        return xtaps.at[field] if field < STEPS else htaps.at[field % 2]
 
     def remote(field, n, src, dst, r, c):
         return pltpu.make_async_remote_copy(
@@ -196,8 +196,7 @@
         slot = slot_of(field)
         for g in range(ROWS * SEQS):
             stage[slot, k, pl.ds((g + SEQS) * PITCH + 8, 8), :] = values[g]
-        if field == 0 or field >= STEPS:
-            field_taps(field)[16 : 16 + CELLS, shift_lanes(1, k)] = values.reshape(CELLS, LANES).astype(BF16)
+        field_taps(field)[16 : 16 + CELLS, shift_lanes(1, k)] = values.reshape(CELLS, LANES).astype(BF16)
         begin = SEQS * PITCH + 8
         last = stage[slot, k, pl.ds(begin + COLS - 1, ROWS * SEQS, stride=PITCH), :]
         first = stage[slot, k, pl.ds(begin, ROWS * SEQS, stride=PITCH), :]
@@ -225,7 +224,7 @@
             for side, g0 in ((0, 0), (1, GROUPS - SEQS)):
                 for s in range(SEQS):
                     stage[slot, k, pl.ds((g0 + s) * PITCH + 8, 8), :] = recv_row[field, side, s, :, lanes].astype(F32)
-            for y in (0, ROWS + 1) if field == 0 or field >= STEPS else range(ROWS + 2):
+            for y in (0, ROWS + 1):
                 shifted(field, y, 1, k)
 
     def build_sides(field):
@@ -284,13 +283,21 @@
     greeted()
     send(0)
     send(STEPS)
-    loaded("own_x", taps_like(wx, 1))
-    loaded("own_h", taps_like(wh, 1))
     loaded("frame1", frames.at[1])
-    for block in range(CHUNKS):
-        gates[0, block] = product(0, block, x_own + h_own)
     prepare(1)
     send(1)
+    loaded("own_x", taps_like(wx, 1))
+    loaded("frames", frames.at[pl.ds(2, 2)])
+    prepare(2)
+    prepare(3)
+    for t in range(1, STEPS):
+        for block in range(CHUNKS):
+            gates[t, block] = product(t, block, x_own)
+    loaded("own_h", taps_like(wh, 1))
+    for block in range(CHUNKS):
+        gates[0, block] = product(0, block, x_own + h_own)
+    send(2)
+    send(3)
     loaded("near_x", taps_like(wx, 2))
     rows_arrived(0)
     build_rows(0)
@@ -302,45 +309,38 @@
     for block in range(CHUNKS):
         add(0, block, x_side[:12])
     loaded("last_x", taps_like(wx, 2))
-    for block in range(CHUNKS):
-        add(0, block, x_side[12:])
-    loaded("frames", frames.at[pl.ds(2, 2)])
     rows_arrived(1)
     sides_arrived(1)
+    for block in range(CHUNKS):
+        add(0, block, x_side[12:])
     build_rows(1)
     build_sides(1)
     for block in range(CHUNKS):
-        gates[1, block] = product(1, block, x_all[:16])
-    prepare(2)
-    prepare(3)
-    send(2)
-    send(3)
+        add(1, block, x_all[:12])
     loaded("cell", cell)
     loaded("bias", bias)
     loaded("most_h", taps_like(wh, 6))
+    loaded("last_h", taps_like(wh, 2))
     rows_arrived(STEPS)
     sides_arrived(STEPS)
+    rows_arrived(2)
+    sides_arrived(2)
     build_rows(STEPS)
     build_sides(STEPS)
-    for block in range(CHUNKS):
-        add(0, block, h_vertical + h_side[:12])
-    loaded("last_h", taps_like(wh, 2))
-    for block in range(CHUNKS):
-        cell_update(0, block, gates[0, block] + product(0, block, h_side[12:]))
+    build_rows(2)
+    build_sides(2)
+    for block in range(CHUNKS):
+        cell_update(0, block, gates[0, block] + product(0, block, h_vertical + h_side))
     send(STEPS + 1)
 
-    rest = {1: x_all[16:], 2: x_all[12:], 3: x_all[6:]}
-    ahead = {1: x_all[:12], 2: x_all[:6]}
+    rest = {1: x_all[12:] + h_own, 2: x_all[8:] + h_own, 3: x_all[4:] + h_own}
+    ahead = {1: x_all[:8], 2: x_all[:4]}
     for t in range(1, STEPS):
         if t in ahead:
-            rows_arrived(t + 1)
-            sides_arrived(t + 1)
-            build_rows(t + 1)
-            build_sides(t + 1)
             for block in range(CHUNKS):
-                gates[t + 1, block] = product(t + 1, block, ahead[t])
+                add(t + 1, block, ahead[t])
         for block in range(CHUNKS):
-            add(t, block, rest[t] + x_own + h_own)
+            add(t, block, rest[t])
         rows_arrived(STEPS + t)
         build_rows(STEPS + t)
         for block in range(CHUNKS):
@@ -348,7 +348,13 @@
         sides_arrived(STEPS + t)
         if t + 1 == STEPS:
             all_sent()
+        if t + 2 < STEPS:
+            rows_arrived(t + 2)
+            sides_arrived(t + 2)
         build_sides(STEPS + t)
+        if t + 2 < STEPS:
+            build_rows(t + 2)
+            build_sides(t + 2)
         for block in range(CHUNKS):
             cell_update(t, block, gates[t, block] + product(t, block, h_side))
         if t + 1 < STEPS:
@@ -386,7 +392,7 @@
                 pltpu.VMEM((GATES,), F32),
                 pltpu.VMEM((STEPS,) + tile, BF16),
                 pltpu.VMEM(tile, BF16),
-                pltpu.VMEM((2, (ROWS + 2) * 16, TAP_ROWS), BF16),
+                pltpu.VMEM((STEPS, (ROWS + 2) * 16, TAP_ROWS), BF16),
                 pltpu.VMEM((2, (ROWS + 2) * 16, TAP_ROWS), BF16),
                 pltpu.VMEM((STEPS, CHUNKS, CELLS, 4 * LANES), F32),
                 pltpu.VMEM((STEPS + 1, CHUNKS, STAGE_ROWS, LANES), F32),

time: 32.3 us -> 31.3 us (0.969)
  Pallas kernels: 31.4 us -> 30.4 us
    pallas_call x1, Pallas kernels: 30.3 us -> 29.3 us  [local_run(): pl.pallas_call(functools.partial(kernel, row_count), out_shape=(pltpu.VME...]
where the time goes in v4:
time: 31.3 us; the launch traced here: 31.2 us
  Pallas kernels  30.4 us (97%)
  between operations  0.8 us (3%)
    pallas_call x1, Pallas kernels, local_run(): pl.pallas_call(functools.partial(kernel, row_count), out_shape=(pltpu.VME...  29.3 us
    pallas_call x1, Pallas kernels, local_run(): pl.pallas_call(write_out, out_shape=(jax.ShapeDtypeStruct(frames.shape, B...  1.09 us

profile of v4, /device:TPU:0, one launch (start us, length us, event | category | flops | bytes accessed | tf_op | source)
XLA Modules:
  0.0 31.2 jit_solution(13155186415179062971)
XLA Ops:
  0.6 29.3 %shard_map.77 = (bf16[4,16,2,8,384]{4,3,2,1,0:T(8,128)(2,1)S(1)}, f32[16,2,8,384]{3,2,1,0:T(8,128)S(1)}) custom-call(bf16[4,2,16,8,384]{4,3,2,1,0:T(8,128)(2,1)} %frames_hbm.1, bf16[3456,1536]{1,0:T(8,128)(2,1)} %bitcast.2, bf16[3456,1536]{1,0:T(8,128)(2,1)} %bitcast.3, f32[1536]{0:T(1024)} %bias_hbm.1, bf16[2,16,8,384]{3,2,1,0:T(8,128)(2,1)} %h_hbm.1, ...), custom_call_target="tpu_custom_call" | custom-call | tf_op jit(solution)/shard_map/pallas_call | solution.py:384
  29.9 1.1 %shard_map.78 = (bf16[4,2,16,8,384]{4,3,2,1,0:T(8,128)(2,1)}, f32[2,16,8,384]{3,2,1,0:T(8,128)}) custom-call(bf16[4,16,2,8,384]{4,3,2,1,0:T(8,128)(2,1)S(1)} %get-tuple-element.4.hidden, f32[16,2,8,384]{3,2,1,0:T(8,128)S(1)} %get-tuple-element.5.cell), custom_call_target="tpu_custom_call" | custom-call | tf_op jit(solution)/shard_map/pallas_call | solution.py:410

commit v5 on v4

--- a/solution.py
+++ b/solution.py
@@ -141,20 +141,23 @@
             down_side=remote(field, 4, send_cor.at[field, 1], recv_cor.at[field, 0], row + 1, other),
         )
 
-    def send(field):
+    def send(field, names=("up_side", "up", "down_side", "down", "side")):
         out = copies(field)
 
         @pl.when(has_up)
         def _():
-            out["up_side"].start()
-            out["up"].start()
+            for name in names:
+                if name.startswith("up"):
+                    out[name].start()
 
         @pl.when(has_down)
         def _():
-            out["down_side"].start()
-            out["down"].start()
-
-        out["side"].start()
+            for name in names:
+                if name.startswith("down"):
+                    out[name].start()
+
+        if "side" in names:
+            out["side"].start()
 
     def pair_arrived(field, n, both):
         @pl.when(inner)
@@ -277,27 +280,28 @@
         gates[t, block] += product(t, block, parts)
 
     loaded("frame0", frames.at[0])
+    greeted()
+    send(0, ("up", "down"))
     prepare(0)
+    send(0, ("up_side", "down_side", "side"))
     loaded("state", h_start)
     prepare(STEPS)
-    greeted()
-    send(0)
     send(STEPS)
     loaded("frame1", frames.at[1])
     prepare(1)
     send(1)
-    loaded("own_x", taps_like(wx, 1))
     loaded("frames", frames.at[pl.ds(2, 2)])
     prepare(2)
+    send(2)
     prepare(3)
+    send(3)
+    loaded("own_x", taps_like(wx, 1))
+    loaded("own_h", taps_like(wh, 1))
     for t in range(1, STEPS):
         for block in range(CHUNKS):
-            gates[t, block] = product(t, block, x_own)
-    loaded("own_h", taps_like(wh, 1))
+            gates[t, block] = product(t, block, x_own[:2])
     for block in range(CHUNKS):
         gates[0, block] = product(0, block, x_own + h_own)
-    send(2)
-    send(3)
     loaded("near_x", taps_like(wx, 2))
     rows_arrived(0)
     build_rows(0)
@@ -309,12 +313,14 @@
     for block in range(CHUNKS):
         add(0, block, x_side[:12])
     loaded("last_x", taps_like(wx, 2))
-    rows_arrived(1)
-    sides_arrived(1)
+    for t in (1,):
+        rows_arrived(t)
+        sides_arrived(t)
     for block in range(CHUNKS):
         add(0, block, x_side[12:])
-    build_rows(1)
-    build_sides(1)
+    for t in (1,):
+        build_rows(t)
+        build_sides(t)
     for block in range(CHUNKS):
         add(1, block, x_all[:12])
     loaded("cell", cell)
@@ -333,7 +339,8 @@
         cell_update(0, block, gates[0, block] + product(0, block, h_vertical + h_side))
     send(STEPS + 1)
 
-    rest = {1: x_all[12:] + h_own, 2: x_all[8:] + h_own, 3: x_all[4:] + h_own}
+    own_rest = x_own[2:] + h_own
+    rest = {1: x_all[12:] + own_rest, 2: x_all[8:] + own_rest, 3: x_all[4:] + own_rest}
     ahead = {1: x_all[:8], 2: x_all[:4]}
     for t in range(1, STEPS):
         if t in ahead:

time: 31.3 us -> 31.1 us (level)
  no operation moved by 1% of the time
where the time goes in v5:
time: 31.1 us; the launch traced here: 31 us
  Pallas kernels  30.2 us (97%)
  between operations  0.8 us (3%)
    pallas_call x1, Pallas kernels, local_run(): pl.pallas_call(functools.partial(kernel, row_count), out_shape=(pltpu.VME...  29.1 us
    pallas_call x1, Pallas kernels, local_run(): pl.pallas_call(write_out, out_shape=(jax.ShapeDtypeStruct(frames.shape, B...  1.09 us

profile of v5, /device:TPU:0, one launch (start us, length us, event | category | flops | bytes accessed | tf_op | source)
XLA Modules:
  0.0 31.0 jit_solution(16203323671351651516)
XLA Ops:
  0.6 29.1 %shard_map.77 = (bf16[4,16,2,8,384]{4,3,2,1,0:T(8,128)(2,1)S(1)}, f32[16,2,8,384]{3,2,1,0:T(8,128)S(1)}) custom-call(bf16[4,2,16,8,384]{4,3,2,1,0:T(8,128)(2,1)} %frames_hbm.1, bf16[3456,1536]{1,0:T(8,128)(2,1)} %bitcast.2, bf16[3456,1536]{1,0:T(8,128)(2,1)} %bitcast.3, f32[1536]{0:T(1024)} %bias_hbm.1, bf16[2,16,8,384]{3,2,1,0:T(8,128)(2,1)} %h_hbm.1, ...), custom_call_target="tpu_custom_call" | custom-call | tf_op jit(solution)/shard_map/pallas_call | solution.py:391
  29.7 1.1 %shard_map.78 = (bf16[4,2,16,8,384]{4,3,2,1,0:T(8,128)(2,1)}, f32[2,16,8,384]{3,2,1,0:T(8,128)}) custom-call(bf16[4,16,2,8,384]{4,3,2,1,0:T(8,128)(2,1)S(1)} %get-tuple-element.4.hidden, f32[16,2,8,384]{3,2,1,0:T(8,128)S(1)} %get-tuple-element.5.cell), custom_call_target="tpu_custom_call" | custom-call | tf_op jit(solution)/shard_map/pallas_call | solution.py:417

commit v6 on v5

--- a/solution.py
+++ b/solution.py
@@ -369,12 +369,13 @@
 
 
 def write_out(hidden, cell, out_hbm, c_out_hbm, sem):
-    copies = [pltpu.make_async_copy(hidden.at[t, :, s], out_hbm.at[t, s], sem.at[t, s]) for t in range(STEPS) for s in range(SEQS)]
-    copies += [pltpu.make_async_copy(cell.at[:, s], c_out_hbm.at[s], sem.at[STEPS, s]) for s in range(SEQS)]
-    for copy in copies:
-        copy.start()
-    for copy in copies:
-        copy.wait()
+    for s in range(SEQS):
+        pltpu.make_async_copy(cell.at[:, s], c_out_hbm.at[s], sem.at[0]).start(priority=s)
+    for t in range(STEPS):
+        for s in range(SEQS):
+            pltpu.make_async_copy(hidden.at[t, :, s], out_hbm.at[t, s], sem.at[1]).start(priority=s)
+    pltpu.make_async_copy(cell, cell, sem.at[0]).wait()
+    pltpu.make_async_copy(hidden, hidden, sem.at[1]).wait()
 
 
 def solution(mesh):
@@ -419,7 +420,7 @@
             out_shape=(jax.ShapeDtypeStruct(frames.shape, BF16), jax.ShapeDtypeStruct(c_init.shape, F32)),
             in_specs=[vmem, vmem],
             out_specs=(hbm, hbm),
-            scratch_shapes=[pltpu.SemaphoreType.DMA((STEPS + 1, SEQS))],
+            scratch_shapes=[pltpu.SemaphoreType.DMA((2,))],
         )(*(pltpu.with_memory_space_constraint(a, pltpu.VMEM) for a in (hidden, cell)))
 
     return jax.shard_map(local_run, mesh=mesh, in_specs=(frame_spec, P(), P(), P(), state_spec, state_spec), out_specs=(frame_spec, state_spec), check_vma=False)

time: 31.1 us -> 31 us (level)
  no operation moved by 1% of the time
where the time goes in v6:
time: 31 us; the launch traced here: 30.9 us
  Pallas kernels  30.1 us (97%)
  between operations  0.8 us (3%)
    pallas_call x1, Pallas kernels, local_run(): pl.pallas_call(functools.partial(kernel, row_count), out_shape=(pltpu.VME...  29.1 us
    pallas_call x1, Pallas kernels, local_run(): pl.pallas_call(write_out, out_shape=(jax.ShapeDtypeStruct(frames.shape, B...  1.01 us

profile of v6, /device:TPU:0, one launch (start us, length us, event | category | flops | bytes accessed | tf_op | source)
XLA Modules:
  0.0 30.9 jit_solution(13996793978202450089)
XLA Ops:
  0.6 29.1 %shard_map.77 = (bf16[4,16,2,8,384]{4,3,2,1,0:T(8,128)(2,1)S(1)}, f32[16,2,8,384]{3,2,1,0:T(8,128)S(1)}) custom-call(bf16[4,2,16,8,384]{4,3,2,1,0:T(8,128)(2,1)} %frames_hbm.1, bf16[3456,1536]{1,0:T(8,128)(2,1)} %bitcast.2, bf16[3456,1536]{1,0:T(8,128)(2,1)} %bitcast.3, f32[1536]{0:T(1024)} %bias_hbm.1, bf16[2,16,8,384]{3,2,1,0:T(8,128)(2,1)} %h_hbm.1, ...), custom_call_target="tpu_custom_call" | custom-call | tf_op jit(solution)/shard_map/pallas_call | solution.py:392
  29.7 1.0 %shard_map.78 = (bf16[4,2,16,8,384]{4,3,2,1,0:T(8,128)(2,1)}, f32[2,16,8,384]{3,2,1,0:T(8,128)}) custom-call(bf16[4,16,2,8,384]{4,3,2,1,0:T(8,128)(2,1)S(1)} %get-tuple-element.4.hidden, f32[16,2,8,384]{3,2,1,0:T(8,128)S(1)} %get-tuple-element.5.cell), custom_call_target="tpu_custom_call" | custom-call | tf_op jit(solution)/shard_map/pallas_call | solution.py:418

commit v7 on v6

--- a/solution.py
+++ b/solution.py
@@ -143,6 +143,8 @@
 
     def send(field, names=("up_side", "up", "down_side", "down", "side")):
         out = copies(field)
+        if "side" in names:
+            out["side"].start()
 
         @pl.when(has_up)
         def _():
@@ -156,8 +158,6 @@
                 if name.startswith("down"):
                     out[name].start()
 
-        if "side" in names:
-            out["side"].start()
 
     def pair_arrived(field, n, both):
         @pl.when(inner)

time: 31 us -> 31.1 us (level)
  no operation moved by 1% of the time
where the time goes in v7:
time: 31.1 us; the launch traced here: 31 us
  Pallas kernels  30.2 us (97%)
  between operations  0.8 us (3%)
    pallas_call x1, Pallas kernels, local_run(): pl.pallas_call(functools.partial(kernel, row_count), out_shape=(pltpu.VME...  29.2 us
    pallas_call x1, Pallas kernels, local_run(): pl.pallas_call(write_out, out_shape=(jax.ShapeDtypeStruct(frames.shape, B...  1.01 us

profile of v7, /device:TPU:0, one launch (start us, length us, event | category | flops | bytes accessed | tf_op | source)
XLA Modules:
  0.0 31.0 jit_solution(8557569720982215136)
XLA Ops:
  0.6 29.2 %shard_map.77 = (bf16[4,16,2,8,384]{4,3,2,1,0:T(8,128)(2,1)S(1)}, f32[16,2,8,384]{3,2,1,0:T(8,128)S(1)}) custom-call(bf16[4,2,16,8,384]{4,3,2,1,0:T(8,128)(2,1)} %frames_hbm.1, bf16[3456,1536]{1,0:T(8,128)(2,1)} %bitcast.2, bf16[3456,1536]{1,0:T(8,128)(2,1)} %bitcast.3, f32[1536]{0:T(1024)} %bias_hbm.1, bf16[2,16,8,384]{3,2,1,0:T(8,128)(2,1)} %h_hbm.1, ...), custom_call_target="tpu_custom_call" | custom-call | tf_op jit(solution)/shard_map/pallas_call | solution.py:392
  29.9 1.0 %shard_map.78 = (bf16[4,2,16,8,384]{4,3,2,1,0:T(8,128)(2,1)}, f32[2,16,8,384]{3,2,1,0:T(8,128)}) custom-call(bf16[4,16,2,8,384]{4,3,2,1,0:T(8,128)(2,1)S(1)} %get-tuple-element.4.hidden, f32[16,2,8,384]{3,2,1,0:T(8,128)S(1)} %get-tuple-element.5.cell), custom_call_target="tpu_custom_call" | custom-call | tf_op jit(solution)/shard_map/pallas_call | solution.py:418
